TPU v7x, 8 devices: a whole 2x2x1 slice. The times are simulated.
8 devices in a mesh: rep: 1 (over z), dp: 8 (over x, y, core).
Axes of the slice: x: 2, y: 2, z: 1, core: 2. Of those that a mesh axis runs over, the one named last changes fastest.
Arguments:
- x: bfloat16 [8, 2048, 1152], P(('rep', 'dp'))
- dy: bfloat16 [8, 2048, 1152], P(('rep', 'dp'))
- w_gate: bfloat16 [2, 1152, 4608], P(None, 'dp')
- w_up: bfloat16 [2, 1152, 4608], P(None, 'dp')
- w_down: bfloat16 [2, 4608, 1152], P(None, 'dp')
- m_w_gate: float32 [2, 1152, 4608], P(None, 'dp')
- m_w_up: float32 [2, 1152, 4608], P(None, 'dp')
- m_w_down: float32 [2, 4608, 1152], P(None, 'dp')
- v_w_gate: float32 [2, 1152, 4608], P(None, 'dp')
- v_w_up: float32 [2, 1152, 4608], P(None, 'dp')
- v_w_down: float32 [2, 4608, 1152], P(None, 'dp')
Outputs:
- output 1: bfloat16 [2, 1152, 4608], P('rep', 'dp')
- output 2: bfloat16 [2, 1152, 4608], P('rep', 'dp')
- output 3: bfloat16 [2, 4608, 1152], P('rep', 'dp')
- output 4: float32 [2, 1152, 4608], P('rep', 'dp')
- output 5: float32 [2, 1152, 4608], P('rep', 'dp')
- output 6: float32 [2, 4608, 1152], P('rep', 'dp')
- output 7: float32 [2, 1152, 4608], P('rep', 'dp')
- output 8: float32 [2, 1152, 4608], P('rep', 'dp')
- output 9: float32 [2, 4608, 1152], P('rep', 'dp')
All inputs are finite; a program needn't handle non-finite values.
Results may differ from a plain program's by a relative error of at most 0.022.
Values are sent between devices in bfloat16 or wider.
A program may use at most 2 GiB of HBM per device.

v0:
```python
import jax
import jax.numpy as jnp
from jax import lax
from jax.sharding import PartitionSpec as P

NAMES = ("w_gate", "w_up", "w_down")


def matmul(a, w):
    return jnp.dot(a, w, preferred_element_type=jnp.float32).astype(jnp.bfloat16)


def normed(h):
    wide = h.astype(jnp.float32)
    scale = lax.rsqrt(jnp.mean(wide**2, -1, keepdims=True) + 1e-6)
    return (wide * scale).astype(jnp.bfloat16)


def layer(h, w):
    a = normed(h)
    gate = jnp.dot(a, w["w_gate"], preferred_element_type=jnp.float32)
    up = jnp.dot(a, w["w_up"], preferred_element_type=jnp.float32)
    return h + matmul((jax.nn.silu(gate) * up).astype(jnp.bfloat16), w["w_down"])


def adamw(w, m, v, g):
    m = 0.9 * m + 0.1 * g
    v = 0.95 * v + 0.05 * g * g
    step = m * lax.rsqrt(v + 1e-8) + 0.1 * w
    return (w - 0.02 * step).astype(jnp.bfloat16), m, v


def solution(mesh):
    def fetched(weights, number):
        return {name: lax.all_gather(w[number], "dp", axis=0, tiled=True) for name, w in zip(NAMES, weights, strict=True)}

    def step(x, dy, *arrays):
        weights, m, v = (arrays[i : i + 3] for i in (0, 3, 6))
        layers = weights[0].shape[0]
        h, kept = x[0], []
        for number in range(layers):
            kept.append(h)
            h = layer(h, fetched(weights, number))
        by_h, mine = dy[0], [None] * layers
        for number in reversed(range(layers)):
            _, back = jax.vjp(lambda w, h: layer(h, w), fetched(weights, number), kept[number])
            by_w, by_h = back(by_h)
            mine[number] = [lax.psum_scatter(by_w[name], "dp", scatter_dimension=0, tiled=True) for name in NAMES]
        gradients = [jnp.stack([mine[number][i] for number in range(layers)]).astype(jnp.float32) for i in range(3)]
        new = [adamw(w.astype(jnp.float32), m, v, g) for w, m, v, g in zip(weights, m, v, gradients, strict=True)]
        return tuple(one[which] for which in range(3) for one in new)

    states, cut = P(("rep", "dp"), None, None), P(None, "dp", None)
    return jax.shard_map(
        step,
        mesh=mesh,
        in_specs=(states, states) + (cut,) * 9,
        out_specs=(P("rep", "dp", None),) * 9,
        check_vma=False,
    )
```

profile of v0, /device:TPU:0, one launch (start us, length us, event | category | flops | bytes accessed | tf_op | source)
XLA Modules:
  0.0 1006.2 jit_solution(1727206753416968955)
XLA Ops:
  7.2 3.5 fusion.97
  10.8 0.0 all-gather.15.cloned.1.call-start
  10.8 3.4 fusion.96
  14.3 0.0 all-gather.17.cloned.1.call-start
  14.3 1.7 fusion.95
  16.1 0.5 all-gather.21.cloned.1.call-update
  16.7 0.5 all-gather.23.cloned.1.call-update
  17.3 0.5 all-gather.19.cloned.1.call-update
  17.8 6.6 copy.20
  24.5 3.3 fusion.34
  27.8 6.6 copy.21
  34.4 37.3 %all-gather.13.cloned.1.call-done = bf16[1,1152,4608]{2,1,0:T(8,128)(2,1)} async-done(((bf16[1,144,4608]{2,1,0:T(8,128)(2,1)}), bf16[1,1152,4608]{2,1,0:T(8,128)(2,1)}) %all-gather.13.cloned.1.call-update) | async-done | bytes 10616848 | tf_op jit(solution)/shard_map/all_gather | solution.py:35
  71.7 32.0 %fusion.32 = f32[2048,4608]{1,0:T(8,128)} fusion(bf16[1,1152,4608]{2,1,0:T(8,128)(2,1)} %all-gather.13.cloned.1.call-done, bf16[1,2048,1152]{1,2,0:T(8,128)(2,1)} %copy.20, f32[2048]{0:T(1024)S(1)} %add_rsqrt_fusion), kind=kOutput, calls=%fused_computation.51 | convolution fusion | flops 21750349824 | bytes 53092352 | tf_op jit(solution)/shard_map/dot_general | solution.py:21
  103.7 28.4 %all-gather.15.cloned.1.call-done = bf16[1,1152,4608]{2,1,0:T(8,128)(2,1)} async-done(((bf16[1,144,4608]{2,1,0:T(8,128)(2,1)}), bf16[1,1152,4608]{2,1,0:T(8,128)(2,1)}) %all-gather.15.cloned.1.call-update) | async-done | bytes 10616848 | tf_op jit(solution)/shard_map/all_gather | solution.py:35
  132.1 45.7 %multiply_convert_fusion.1 = (bf16[2048,4608]{1,0:T(8,128)(2,1)}, f32[2048,4608]{1,0:T(8,128)}) fusion(f32[2048,4608]{1,0:T(8,128)} %fusion.32, bf16[1,1152,4608]{2,1,0:T(8,128)(2,1)} %all-gather.15.cloned.1.call-done, bf16[1,2048,1152]{1,2,0:T(8,128)(2,1)} %copy.20, f32[2048]{0:T(1024)S(1)} %add_rsqrt_fusion), kind=kOutput, calls=%fused_computation.17 | convolution fusion | flops 21806972928 | bytes 109715456 | tf_op jit(solution)/shard_map/dot_general | solution.py:22
  177.8 14.7 %all-gather.17.cloned.1.call-done = bf16[1,4608,1152]{2,1,0:T(8,128)(2,1)} async-done(((bf16[1,576,1152]{2,1,0:T(8,128)(2,1)}), bf16[1,4608,1152]{2,1,0:T(8,128)(2,1)}) %all-gather.17.cloned.1.call-update) | async-done | bytes 10616848 | tf_op jit(solution)/shard_map/all_gather | solution.py:35
  192.5 30.7 %fusion.38 = (f32[2048]{0:T(1024)S(1)}, bf16[2048,1152]{0,1:T(8,128)(2,1)}) fusion(bf16[2048,4608]{1,0:T(8,128)(2,1)} %get-tuple-element.24, bf16[1,4608,1152]{2,1,0:T(8,128)(2,1)} %all-gather.17.cloned.1.call-done, bf16[1,2048,1152]{1,2,0:T(8,128)(2,1)} %copy.20), kind=kOutput, calls=%fused_computation.57 | convolution fusion | flops 21755066368 | bytes 38936576 | tf_op jit(solution)/shard_map/dot_general | solution.py:10
  223.2 29.5 %all-gather.21.cloned.1.call-done = bf16[1,4608,1152]{2,1,0:T(8,128)(2,1)} async-done(((bf16[1,576,1152]{2,1,0:T(8,128)(2,1)}), bf16[1,4608,1152]{2,1,0:T(8,128)(2,1)}) %all-gather.21.cloned.1.call-update) | async-done | bytes 10616848 | tf_op jit(solution)/shard_map/all_gather | solution.py:35
  252.7 31.7 %convolution_convert_fusion.1 = bf16[2048,4608]{1,0:T(8,128)(2,1)} fusion(bf16[1,4608,1152]{2,1,0:T(8,128)(2,1)} %all-gather.21.cloned.1.call-done, bf16[1,2048,1152]{2,1,0:T(8,128)(2,1)} %param.12), kind=kOutput, calls=%fused_computation.26 | convolution fusion | flops 21752709120 | bytes 34209792 | tf_op jit(solution)/shard_map/transpose(jvp())/dot_general | solution.py:10
  284.4 28.5 %all-gather.23.cloned.1.call-done = bf16[1,1152,4608]{2,1,0:T(8,128)(2,1)} async-done(((bf16[1,144,4608]{2,1,0:T(8,128)(2,1)}), bf16[1,1152,4608]{2,1,0:T(8,128)(2,1)}) %all-gather.23.cloned.1.call-update) | async-done | bytes 10616848 | tf_op jit(solution)/shard_map/all_gather | solution.py:35
  312.9 32.0 %fusion.19 = f32[2048,4608]{1,0:T(8,128)} fusion(bf16[1,1152,4608]{2,1,0:T(8,128)(2,1)} %all-gather.23.cloned.1.call-done, bf16[2048,1152]{0,1:T(8,128)(2,1)} %get-tuple-element.27, f32[2048]{0:T(1024)S(1)} %fusion.83), kind=kOutput, calls=%fused_computation.38 | convolution fusion | flops 21750349824 | bytes 53092352 | tf_op jit(solution)/shard_map/jvp()/dot_general | solution.py:22
  344.9 28.2 %all-gather.19.cloned.1.call-done = bf16[1,1152,4608]{2,1,0:T(8,128)(2,1)} async-done(((bf16[1,144,4608]{2,1,0:T(8,128)(2,1)}), bf16[1,1152,4608]{2,1,0:T(8,128)(2,1)}) %all-gather.19.cloned.1.call-update) | async-done | bytes 10616848 | tf_op jit(solution)/shard_map/all_gather | solution.py:35
  373.2 52.7 %fusion.2 = (bf16[2048,4608]{1,0:T(8,128)(2,1)}, f32[2048,4608]{1,0:T(8,128)}) fusion(f32[2048,4608]{1,0:T(8,128)} %fusion.19, bf16[2048,4608]{1,0:T(8,128)(2,1)} %convolution_convert_fusion.1, bf16[1,1152,4608]{2,1,0:T(8,128)(2,1)} %all-gather.19.cloned.1.call-done, bf16[2048,1152]{0,1:T(8,128)(2,1)} %get-tuple-element.27, f32[2048]{0:T(1024)S(1)} %fusion.83), kind=kOutput, calls=%fused_computation.8 | convolution fusion | flops 21863596032 | bytes 128589824 | tf_op jit(solution)/shard_map/jvp()/dot_general | solution.py:21
  425.8 29.3 %fusion.44 = bf16[2048,1152]{0,1:T(8,128)(2,1)} fusion(bf16[2048,4608]{1,0:T(8,128)(2,1)} %get-tuple-element.28, bf16[1,1152,4608]{2,1,0:T(8,128)(2,1)} %all-gather.19.cloned.1.call-done), kind=kOutput, calls=%fused_computation.64 | convolution fusion | flops 21743271936 | bytes 34209792 | tf_op jit(solution)/shard_map/transpose(jvp())/dot_general | solution.py:21
  455.2 38.3 %fusion.40 = (f32[2048]{0:T(1024)S(1)}, bf16[2048,1152]{0,1:T(8,128)(2,1)}) fusion(bf16[2048,1152]{0,1:T(8,128)(2,1)} %get-tuple-element.27, bf16[2048,1152]{0,1:T(8,128)(2,1)} %fusion.44, bf16[1,1152,4608]{2,1,0:T(8,128)(2,1)} %all-gather.23.cloned.1.call-done, bf16[2048,4608]{1,0:T(8,128)(2,1)} %convolution_convert_fusion.1, ...), kind=kOutput, calls=%fused_computation.59 | convolution fusion | flops 21814048768 | bytes 81403904 | tf_op jit(solution)/shard_map/transpose(jvp())/dot_general | solution.py:22
  493.4 8.6 fusion.72
  502.1 2.2 copy-done.3
  504.3 29.6 %convolution_convert_fusion.3 = bf16[4608,1152]{1,0:T(8,128)(2,1)} fusion(bf16[2048,4608]{1,0:T(8,128)(2,1)} %get-tuple-element.24, bf16[2048,1152]{0,1:T(8,128)(2,1)S(1)} %fusion.72), kind=kOutput, calls=%fused_computation.28 | convolution fusion | flops 21748580352 | bytes 34209792 | tf_op jit(solution)/shard_map/transpose(jvp())/dot_general | solution.py:10
  533.9 0.0 reduce-scatter.17.cloned.1.call-start
  534.0 37.7 %convolution_convert_fusion.2 = bf16[4608,1152]{1,0:T(8,128)(2,1)} fusion(f32[2048,4608]{1,0:T(8,128)} %fusion.19, bf16[1,2048,1152]{2,1,0:T(8,128)(2,1)} %param.12, f32[2048,4608]{1,0:T(8,128)} %get-tuple-element.29), kind=kOutput, calls=%fused_computation.27 | convolution fusion | flops 21805203456 | bytes 90832896 | tf_op jit(solution)/shard_map/transpose(jvp())/dot_general | solution.py:10
  571.7 0.0 reduce-scatter.11.cloned.1.call-start
  571.8 31.7 %convolution_convert_fusion = bf16[2048,4608]{1,0:T(8,128)(2,1)} fusion(bf16[2048,1152]{0,1:T(8,128)(2,1)} %copy-done.3, bf16[1,4608,1152]{2,1,0:T(8,128)(2,1)} %all-gather.17.cloned.1.call-done), kind=kOutput, calls=%fused_computation.25 | convolution fusion | flops 21752709120 | bytes 34209792 | tf_op jit(solution)/shard_map/transpose(jvp())/dot_general | solution.py:10
  603.5 34.5 %fusion.17 = bf16[1152,4608]{1,0:T(8,128)(2,1)} fusion(bf16[2048,4608]{1,0:T(8,128)(2,1)} %convolution_convert_fusion, f32[2048,4608]{1,0:T(8,128)} %fusion.32, bf16[1,2048,1152]{1,2,0:T(8,128)(2,1)} %copy.20, f32[2048]{0:T(1024)S(1)} %copy-done.9), kind=kOutput, calls=%fused_computation.24 | convolution fusion | flops 21812281344 | bytes 71966720 | tf_op jit(solution)/shard_map/transpose(jvp())/dot_general | solution.py:22
  638.0 0.0 reduce-scatter.13.cloned.1.call-start
  638.0 0.6 copy-done.5
  638.6 34.7 %fusion.13 = bf16[1152,4608]{1,0:T(8,128)(2,1)} fusion(bf16[2048,4608]{1,0:T(8,128)(2,1)} %convolution_convert_fusion.1, bf16[2048,1152]{0,1:T(8,128)(2,1)} %get-tuple-element.27, f32[2048]{0:T(1024)S(1)} %copy-done.5, f32[2048,4608]{1,0:T(8,128)} %get-tuple-element.29), kind=kOutput, calls=%fused_computation.22 | convolution fusion | flops 21812281344 | bytes 71966720 | tf_op jit(solution)/shard_map/transpose(jvp())/dot_general | solution.py:22
  673.4 0.0 reduce-scatter.7.cloned.1.call-start
  673.5 41.9 %fusion.14 = bf16[1152,4608]{1,0:T(8,128)(2,1)} fusion(f32[2048,4608]{1,0:T(8,128)} %fusion.32, f32[2048,4608]{1,0:T(8,128)} %get-tuple-element.25, bf16[2048,4608]{1,0:T(8,128)(2,1)} %convolution_convert_fusion, bf16[1,2048,1152]{1,2,0:T(8,128)(2,1)} %copy.20, f32[2048]{0:T(1024)S(1)} %copy-done.9), kind=kOutput, calls=%fused_computation.23 | convolution fusion | flops 21859467264 | bytes 109715456 | tf_op jit(solution)/shard_map/transpose(jvp())/dot_general | solution.py:21
  715.4 0.0 reduce-scatter.9.cloned.1.call-start
  715.4 29.0 %convolution_convert_fusion.4 = bf16[1152,4608]{1,0:T(8,128)(2,1)} fusion(bf16[2048,4608]{1,0:T(8,128)(2,1)} %get-tuple-element.28, bf16[2048,1152]{0,1:T(8,128)(2,1)} %get-tuple-element.27, f32[2048]{0:T(1024)S(1)} %copy-done.5), kind=kOutput, calls=%fused_computation.29 | convolution fusion | flops 21750349824 | bytes 34217984 | tf_op jit(solution)/shard_map/transpose(jvp())/dot_general | solution.py:21
  744.4 1.7 copy-done.1
  746.1 9.2 fusion.67
  755.4 5.1 reduce-scatter.11.cloned.1.call-done
  760.5 76.3 %reduce-scatter.13.cloned.1.call-done = bf16[144,4608]{1,0:T(8,128)(2,1)} async-done(((bf16[1152,4608]{1,0:T(8,128)(2,1)}), bf16[144,4608]{1,0:T(8,128)(2,1)}) %reduce-scatter.13.cloned.1.call-update) | async-done | bytes 1327120 | tf_op jit(solution)/shard_map/reduce_scatter | solution.py:48
  836.8 9.8 fusion.63
  846.6 66.7 %reduce-scatter.7.cloned.1.call-done = bf16[144,4608]{1,0:T(8,128)(2,1)} async-done(((bf16[1152,4608]{1,0:T(8,128)(2,1)}), bf16[144,4608]{1,0:T(8,128)(2,1)}) %reduce-scatter.7.cloned.1.call-update) | async-done | bytes 1327120 | tf_op jit(solution)/shard_map/reduce_scatter | solution.py:48
  913.3 76.4 %reduce-scatter.9.cloned.1.call-done = bf16[144,4608]{1,0:T(8,128)(2,1)} async-done(((bf16[1152,4608]{1,0:T(8,128)(2,1)}), bf16[144,4608]{1,0:T(8,128)(2,1)}) %reduce-scatter.9.cloned.1.call-update) | async-done | bytes 1327120 | tf_op jit(solution)/shard_map/reduce_scatter | solution.py:48
  989.7 9.2 fusion.59
  (36 shorter events, 0.4 us)
Async XLA Ops:
  7.2 7.1 copy-start
  7.2 64.6 %all-gather.13.cloned.1.call-start = ((), (), s32[]{:S(2)}) async-start(), calls=%async_computation.12 | async-start | bytes 11943936 | tf_op jit(solution)/shard_map/all_gather | solution.py:35
  10.8 121.3 %all-gather.15.cloned.1.call-start = ((), (), s32[]{:S(2)}) async-start(), calls=%async_computation.13 | async-start | bytes 11943936 | tf_op jit(solution)/shard_map/all_gather | solution.py:35
  14.3 178.2 %all-gather.17.cloned.1.call-start = ((), (), s32[]{:S(2)}) async-start(), calls=%async_computation.14 | async-start | bytes 11943936 | tf_op jit(solution)/shard_map/all_gather | solution.py:35
  16.1 236.7 %all-gather.21.cloned.1.call-start = ((), (), s32[]{:S(2)}) async-start(), calls=%async_computation.16 | async-start | bytes 11943936 | tf_op jit(solution)/shard_map/all_gather | solution.py:35
  16.6 296.3 %all-gather.23.cloned.1.call-start = ((), (), s32[]{:S(2)}) async-start(), calls=%async_computation.17 | async-start | bytes 11943936 | tf_op jit(solution)/shard_map/all_gather | solution.py:35
  17.2 355.9 %all-gather.19.cloned.1.call-start = ((), (), s32[]{:S(2)}) async-start(), calls=%async_computation.15 | async-start | bytes 11943936 | tf_op jit(solution)/shard_map/all_gather | solution.py:35
  17.8 726.6 %reduce-scatter.15.cloned.1.call-start = ((), (), s32[]{:S(2)}) async-start(), calls=%async_computation.10 | async-start | bytes 11943936 | tf_op jit(solution)/shard_map/reduce_scatter | solution.py:48
  27.8 104.3 %copy-start.8 = (f32[2048]{0:T(1024)}, f32[2048]{0:T(1024)S(1)}, u32[]{:S(2)}) copy-start(f32[2048]{0:T(1024)S(1)} %add_rsqrt_fusion) | copy-start | bytes 24580
  223.2 61.3 %copy-start.6 = (f32[2048]{0:T(1024)}, f32[2048]{0:T(1024)S(1)}, u32[]{:S(2)}) copy-start(f32[2048]{0:T(1024)S(1)} %get-tuple-element.26) | copy-start | bytes 24580
  223.2 270.3 %copy-start.4 = (f32[2048]{0:T(1024)}, f32[2048]{0:T(1024)S(1)}, u32[]{:S(2)}) copy-start(f32[2048]{0:T(1024)S(1)} %fusion.83) | copy-start | bytes 24580
  455.2 38.3 %copy-start.7 = (f32[2048]{0:T(1024)S(1)}, f32[2048]{0:T(1024)}, u32[]{:S(2)}) copy-start(f32[2048]{0:T(1024)} %copy-done.6) | copy-start | bytes 24580
  502.1 2.2 copy-start.3
  533.9 210.5 %reduce-scatter.17.cloned.1.call-start = ((), (), s32[]{:S(2)}) async-start(), calls=%async_computation.11 | async-start | bytes 11943936 | tf_op jit(solution)/shard_map/reduce_scatter | solution.py:48
  571.7 31.7 %copy-start.9 = (f32[2048]{0:T(1024)S(1)}, f32[2048]{0:T(1024)}, u32[]{:S(2)}) copy-start(f32[2048]{0:T(1024)} %copy-done.8) | copy-start | bytes 24580
  571.7 188.7 %reduce-scatter.11.cloned.1.call-start = ((), (), s32[]{:S(2)}) async-start(), calls=%async_computation.8 | async-start | bytes 11943936 | tf_op jit(solution)/shard_map/reduce_scatter | solution.py:48
  637.9 0.7 copy-start.5
  638.0 198.8 %reduce-scatter.13.cloned.1.call-start = ((), (), s32[]{:S(2)}) async-start(), calls=%async_computation.9 | async-start | bytes 11943936 | tf_op jit(solution)/shard_map/reduce_scatter | solution.py:48
  673.4 239.9 %reduce-scatter.7.cloned.1.call-start = ((), (), s32[]{:S(2)}) async-start(), calls=%async_computation.6 | async-start | bytes 11943936 | tf_op jit(solution)/shard_map/reduce_scatter | solution.py:48
  715.4 274.3 %reduce-scatter.9.cloned.1.call-start = ((), (), s32[]{:S(2)}) async-start(), calls=%async_computation.7 | async-start | bytes 11943936 | tf_op jit(solution)/shard_map/reduce_scatter | solution.py:48
  744.4 1.7 copy-start.1
  836.8 152.9 %copy-start.2 = (bf16[2,144,4608]{2,1,0:T(8,128)(2,1)S(1)}, bf16[2,144,4608]{2,1,0:T(8,128)(2,1)}, u32[]{:S(2)}) copy-start(bf16[2,144,4608]{2,1,0:T(8,128)(2,1)} %param.13) | copy-start | bytes 7962628
Sparse Core Ops, SparseCore 0:
  10.9 60.7 all-gather.12
  74.1 57.9 all-gather.14
  134.5 57.9 all-gather.16
  194.7 57.9 all-gather.20
  255.0 57.9 all-gather.22
  315.2 57.9 all-gather.18
  534.1 73.3 reduce-scatter.14
  610.8 73.0 reduce-scatter.16
  687.4 73.0 reduce-scatter.10
  763.7 73.0 reduce-scatter.12
  840.2 73.0 reduce-scatter.6
  916.6 73.0 reduce-scatter.8
where the time goes:
time: 1010 us
  matrix products  531 us (53%)
  waiting for transfers between devices  393 us (39%)
  other arithmetic  40.3 us (4%)
  local copies, waits for them, and re-layouts  26.4 us (3%)
  between operations  14.8 us (1%)
    reduce_scatter x6, waiting for transfers between devices, step(): lax.psum_scatter(by_w[name], 'dp', scatter_dimension=0, tiled=True)  225 us
    dot_general x5, matrix products, layer(): up = jnp.dot(a, w['w_up'], preferred_element_type=jnp.float32)  185 us
    dot_general x5, matrix products, layer(): gate = jnp.dot(a, w['w_gate'], preferred_element_type=jnp.float32)  185 us
    all_gather x6, waiting for transfers between devices, fetched(): lax.all_gather(w[number], 'dp', axis=0, tiled=True)  167 us
    dot_general x5, matrix products, matmul(): jnp.dot(a, w, preferred_element_type=jnp.float32).astype(jnp.bfloat16)  161 us
    convert_element_type x3, other arithmetic, adamw(): return ((w - 0.02 * step).astype(jnp.bfloat16), m, v)  28.3 us
  transfers between devices with their start and end apart: 12, of which 10 were waited for; matrix products, arithmetic and copies ran while one was open for 42% of the time, Pallas kernels for 0%

commit v1 on v0

v1 whole, which is shorter than its diff:
```python
import functools
import math

import jax
import jax.numpy as jnp
from jax import lax
from jax.experimental import pallas as pl
from jax.experimental.pallas import tpu as pltpu
from jax.sharding import PartitionSpec as P

F32, BF16 = jnp.float32, jnp.bfloat16
MESH = pl.DeviceIdType.MESH
ANY = pl.BlockSpec(memory_space=pl.ANY)
PARTS = 3
TILE = 512


def mm(a, w):
    return lax.dot_general(a, w, (((1,), (0,)), ((), ())), preferred_element_type=F32)


def mm_t(a, w):
    return lax.dot_general(a, w, (((1,), (1,)), ((), ())), preferred_element_type=F32)


def t_mm(a, d):
    return lax.dot_general(a, d, (((0,), (0,)), ((), ())), preferred_element_type=F32)


def normed(h):
    wide = h.astype(F32)
    scale = lax.rsqrt(jnp.mean(wide**2, -1, keepdims=True) + 1e-6)
    return (wide * scale).astype(BF16)


def by_normed(h, by_a):
    wide, by = h.astype(F32), by_a.astype(F32)
    scale = lax.rsqrt(jnp.mean(wide**2, -1, keepdims=True) + 1e-6)
    return (scale * by - wide * (scale**3 * jnp.mean(wide * by, -1, keepdims=True))).astype(BF16)


def adamw(w, m, v, g):
    m = 0.9 * m + 0.1 * g
    v = 0.95 * v + 0.05 * g * g
    step = m * lax.rsqrt(v + 1e-8) + 0.1 * w
    return (w - 0.02 * step).astype(BF16), m, v


def other(me, bit):
    return me + bit - 2 * bit * ((me // bit) % 2)


def remote(src, dst, sems, n, bit):
    return pltpu.make_async_remote_copy(
        src_ref=src,
        dst_ref=dst,
        send_sem=sems[0].at[n],
        recv_sem=sems[1].at[n],
        device_id={"dp": other(lax.axis_index("dp"), bit)},
        device_id_type=MESH,
    )


class Gather:
    bits = (2, 4)

    def __init__(self, block):
        _, r, n = block.shape
        self.ins = [block]
        self.outs = [jax.ShapeDtypeStruct((8, r, n), block.dtype)]
        self.scratch = [pltpu.VMEM((2, r, n), block.dtype), pltpu.SemaphoreType.DMA((2,)), pltpu.SemaphoreType.DMA((6,)), pltpu.SemaphoreType.DMA((6,))]

    def bind(self, ins, outs, scratch):
        (block,), (full,), (held, local, *sems) = ins, outs, scratch
        chip = lax.axis_index("dp") // 2
        at = lambda bit, half: full.at[other(chip, bit) * 2 + half] if bit else full.at[chip * 2 + half]
        self.copies = [
            remote(block.at[1], at(0, 1), sems, 0, 2),
            remote(block.at[0], at(0, 0), sems, 1, 4),
            remote(block.at[0], at(0, 0), sems, 2, 2),
            remote(block.at[1], at(0, 1), sems, 3, 4),
            remote(at(2, 0), at(2, 0), sems, 4, 2),
            remote(at(1, 1), at(1, 1), sems, 5, 4),
        ]
        self.own = [pltpu.make_async_copy(block, held, local.at[0]), pltpu.make_async_copy(held, full.at[pl.ds(chip * 2, 2)], local.at[1])]

    def begin(self):
        for copy in self.copies[:4]:
            copy.start()
        self.own[0].start()

    def middle(self):
        self.own[0].wait()
        self.own[1].start()
        self.copies[1].wait_recv()
        self.copies[4].start()
        self.copies[0].wait_recv()
        self.copies[5].start()

    def late(self):
        pass

    def end(self):
        for n in (2, 3, 4, 5):
            self.copies[n].wait_recv()
        for copy in self.copies:
            copy.wait_send()
        self.own[1].wait()


class Scatter:
    bits = (2, 4)

    def __init__(self, blocks):
        _, r, n = blocks.shape
        self.ins = [blocks]
        self.outs = [jax.ShapeDtypeStruct((2, r, n), BF16)] * 2
        self.scratch = [pltpu.VMEM((2, r, n), BF16)] * 3 + [pltpu.SemaphoreType.DMA((2,)), pltpu.SemaphoreType.DMA((6,)), pltpu.SemaphoreType.DMA((6,))]

    def bind(self, ins, outs, scratch):
        (blocks,), (by_y, by_x), (came, mine, total, local, *sems) = ins, outs, scratch
        chip = lax.axis_index("dp") // 2
        at = lambda bit, half: blocks.at[other(chip, bit) * 2 + half]
        diagonal = lambda half: blocks.at[(3 - chip) * 2 + half]
        self.came, self.mine, self.total = came, mine, total
        self.copies = [
            remote(diagonal(0), came.at[0], sems, 0, 4),
            remote(diagonal(1), came.at[1], sems, 1, 2),
            remote(at(2, 0), by_x.at[0], sems, 2, 4),
            remote(at(1, 1), by_y.at[1], sems, 3, 2),
            remote(total.at[0], by_y.at[0], sems, 4, 2),
            remote(total.at[1], by_x.at[1], sems, 5, 4),
        ]
        self.own = [pltpu.make_async_copy(at(1, 0), mine.at[0], local.at[0]), pltpu.make_async_copy(at(2, 1), mine.at[1], local.at[1])]

    def begin(self):
        for copy in self.copies[:4]:
            copy.start()
        for copy in self.own:
            copy.start()

    def middle(self):
        for half in range(2):
            self.copies[half].wait_recv()
            self.own[half].wait()
            self.total[half] = (self.came[half].astype(F32) + self.mine[half].astype(F32)).astype(BF16)

    def late(self):
        self.copies[4].start()
        self.copies[5].start()

    def end(self):
        for n in (2, 3, 4, 5):
            self.copies[n].wait_recv()
        for copy in self.copies:
            copy.wait_send()


def run(name, cid, compute, grid, ins, in_specs, outs, out_specs, scratch=(), comms=(), bits=(), when=(0.4, 0.5), flops=0):
    steps = math.prod(grid)
    bits = sorted(set(bits).union(*(comm.bits for comm in comms)))
    middle, late = (min(steps - 1, int(steps * w)) for w in when)
    counts = [len(ins)] + [len(c.ins) for c in comms] + [len(outs)] + [len(c.outs) for c in comms] + [len(scratch)] + [len(c.scratch) for c in comms]

    def kernel(*refs):
        refs, groups = list(refs), []
        for count in counts:
            groups.append(refs[:count])
            refs = refs[count:]
        step = 0
        for axis, size in enumerate(grid):
            step = step * size + pl.program_id(axis)
        k = len(comms) + 1
        own = groups[0], groups[k], groups[2 * k]
        for n, comm in enumerate(comms):
            comm.bind(groups[1 + n], groups[k + 1 + n], groups[2 * k + 1 + n])

        @pl.when(step == 0)
        def _():
            if bits:
                barrier = pltpu.get_barrier_semaphore()
                for bit in bits:
                    pl.semaphore_signal(barrier, inc=1, device_id={"dp": other(lax.axis_index("dp"), bit)}, device_id_type=MESH)
                pl.semaphore_wait(barrier, len(bits))
            for comm in comms:
                comm.begin()

        compute(*own)
        for at, what in ((middle, "middle"), (late, "late"), (steps - 1, "end")):
            if comms:

                @pl.when(step == at)
                def _():
                    for comm in comms:
                        getattr(comm, what)()

    params = dict(collective_id=cid, has_side_effects=True) if bits else {}
    results = pl.pallas_call(
        kernel,
        name=name,
        grid=grid,
        in_specs=list(in_specs) + [ANY for c in comms for _ in c.ins],
        out_specs=list(out_specs) + [ANY for c in comms for _ in c.outs],
        out_shape=list(outs) + [o for c in comms for o in c.outs],
        scratch_shapes=list(scratch) + [s for c in comms for s in c.scratch],
        compiler_params=pltpu.CompilerParams(dimension_semantics=("arbitrary",) * len(grid), vmem_limit_bytes=62 * 2**20, **params),
        cost_estimate=pl.CostEstimate(flops=int(flops), bytes_accessed=0, transcendentals=0),
    )(*ins, *[a for c in comms for a in c.ins])
    return results[: len(outs)], results[len(outs) :]


def solution(mesh):
    size = mesh.shape["dp"]
    chips = size // 2
    pairs = [(i, i ^ 1) for i in range(size)]

    def sibling(a):
        return lax.ppermute(a, "dp", pairs)

    def step(x, dy, *arrays):
        weights, m, v = (arrays[i : i + 3] for i in (0, 3, 6))
        first = lax.axis_index("dp") % 2 == 0
        chip = lax.axis_index("dp") // 2
        layers, rows, ff = weights[0].shape
        d = rows * size
        half = ff // 2
        part = half // PARTS
        share = part // chips
        tokens = x.shape[1]
        every = 2 * tokens
        unit = 2 * every * d * half

        def split(w):
            even, odd = jnp.moveaxis(w.reshape(rows, chips, 2, PARTS, share), (2, 3), (0, 2)).reshape(2, rows, half)
            return jnp.where(first, even, odd), jnp.where(first, odd, even)

        def join(mine, theirs):
            both = jnp.stack([jnp.where(first, mine, theirs), jnp.where(first, theirs, mine)])
            return jnp.moveaxis(both.reshape(2, rows, PARTS, chips, share), (0, 2), (2, 3)).reshape(rows, ff)

        def in_order(mine, theirs):
            return jnp.stack([jnp.where(first, mine, theirs), jnp.where(first, theirs, mine)])

        blocks = {}
        for n in range(layers):
            for i in range(2):
                mine, give = split(weights[i][n])
                blocks[i, n] = in_order(mine, sibling(give))
            blocks[2, n] = weights[2][n].reshape(2, -1, d)

        def both(a):
            return jnp.concatenate([a, sibling(a)])

        cid = iter(range(100))
        wide = every // 4
        col, row = lambda n: pl.BlockSpec((wide, n), lambda j, i: (i, 0)), pl.BlockSpec((wide, part), lambda j, i: (i, j))
        weight = pl.BlockSpec((d, part), lambda j, i: (0, j))
        f32_rows, bf16_rows = jax.ShapeDtypeStruct((every, half), F32), jax.ShapeDtypeStruct((every, half), BF16)

        def gate_of(a, w, fetch):
            def compute(ins, outs, _):
                outs[0][...] = mm(ins[0][...], ins[1][...])

            (gate,), (got,) = run("gate", next(cid), compute, (PARTS, 4), [a, w], [col(d), weight], [f32_rows], [row], comms=[Gather(fetch)], flops=unit)
            return gate, got

        def up_of(a, w, gate, fetch):
            def compute(ins, outs, _):
                up, gate = mm(ins[0][...], ins[1][...]), ins[2][...]
                outs[0][...] = up
                outs[1][...] = (jax.nn.silu(gate) * up).astype(BF16)

            (up, hidden), (got,) = run(
                "up", next(cid), compute, (PARTS, 4), [a, w, gate], [col(d), weight, row], [f32_rows, bf16_rows], [row, row], comms=[Gather(fetch)], flops=unit
            )
            return up, hidden, got

        def over_cores(name, terms, lhs, lhs_specs, rhs, given, finish, keep, comms):
            tiles = tokens // TILE
            here = pl.BlockSpec((TILE, d), lambda t: (jnp.maximum(t - tiles, 0), 0))

            def compute(ins, outs, scratch):
                sent, came, state, ssem, rsem, ssem2, rsem2, local = scratch
                t = pl.program_id(0)
                total = terms(ins[: len(lhs)], ins[len(lhs) : len(lhs) + len(rhs)])
                away = lambda n: remote(sent.at[n], came.at[n], (ssem, rsem), n, 1)
                shared = outs[-1]
                rows_of = lambda n: pl.ds(n * TILE, TILE)
                tell = lambda n: remote(state.at[n], shared.at[1, rows_of(n)], (ssem2, rsem2), n, 1)
                save = lambda n: pltpu.make_async_copy(state.at[n], shared.at[0, rows_of(n)], local.at[n])

                for n in range(tiles):

                    @pl.when(t == n)
                    def _():
                        sent[n] = total

                    @pl.when(t == n + 1)
                    def _():
                        away(n).start()

                    @pl.when(t == n + tiles)
                    def _():
                        away(n).wait_recv()
                        results = finish(total + came[n], *[g[...] for g in ins[len(lhs) + len(rhs) :]])
                        for out, result in zip(outs[:-1], results[:-1], strict=True):
                            out[...] = result
                        state[n] = results[-1]
                        if n:
                            tell(n - 1).start()
                            save(n - 1).start()

                @pl.when(t == 2 * tiles - 1)
                def _():
                    tell(tiles - 1).start()
                    save(tiles - 1).start()
                    for n in range(tiles):
                        away(n).wait_send()
                        tell(n).wait()
                        save(n).wait()

            scratch = [pltpu.VMEM((tiles, TILE, d), F32)] * 2 + [pltpu.VMEM((tiles, TILE, d), BF16)] + [pltpu.SemaphoreType.DMA((tiles,))] * 5
            whole = lambda a: pl.BlockSpec(a.shape, lambda t: (0,) * a.ndim, pipeline_mode=pl.Buffered(1))
            results, got = run(
                name,
                next(cid),
                compute,
                (2 * tiles,),
                [*lhs, *rhs, *given],
                list(lhs_specs) + [whole(a) for a in rhs] + [here] * len(given),
                [jax.ShapeDtypeStruct((tokens, d), BF16)] * keep + [jax.ShapeDtypeStruct((2, tokens, d), BF16)],
                [here] * keep + [ANY],
                scratch,
                comms=comms,
                bits=(1,),
                flops=unit * len(lhs),
            )
            return [*results[:-1], results[-1].reshape(every, d)], got

        swapped = lambda n: pl.BlockSpec((TILE, n), lambda t: ((t + tokens // TILE) % (every // TILE), 0))

        def down_of(hidden, w, h, fetch):
            def terms(lhs, rhs):
                return sum(mm(lhs[0][:, p * part : (p + 1) * part], rhs[0][:, p].reshape(part, d)) for p in range(PARTS))

            def finish(total, h):
                h = h + total.astype(BF16)
                return h, normed(h)

            (h, a), (got,) = over_cores("down", terms, [hidden], [swapped(half)], [w.reshape(chips, PARTS, share, d)], [h], finish, 1, [Gather(fetch)])
            return h, a, got

        def by_hidden(p, by_h, w, gate, up, a, keep, comms=()):
            n_steps = every // TILE

            def compute(ins, outs, scratch):
                by_h, w, gate, up, a = (r[...] for r in ins)
                by = mm_t(by_h, w.reshape(part, d)).astype(BF16).astype(F32)
                sig = 1 / (1 + jnp.exp(-gate))
                act = gate * sig
                by_up = (by * act).astype(BF16)
                by_gate = (by * up * (sig * (1 + gate * (1 - sig)))).astype(BF16)
                if keep:
                    outs[3][...], outs[4][...] = by_gate, by_up
                t = pl.program_id(0)
                hidden = (act * up).astype(BF16)
                for acc, lhs, rhs in zip(scratch, (a, a, hidden), (by_gate, by_up, by_h), strict=True):

                    @pl.when(t == 0)
                    def _():
                        acc[...] = t_mm(lhs, rhs)

                    @pl.when(t > 0)
                    def _():
                        acc[...] += t_mm(lhs, rhs)

                @pl.when(t == n_steps - 1)
                def _():
                    for acc, out in zip(scratch, outs[:3], strict=True):
                        out[...] = acc[...].astype(BF16)

            tile = lambda n: pl.BlockSpec((TILE, n), lambda t: (t, 0))
            piece = pl.BlockSpec((TILE, part), lambda t: (t, p))
            whole = lambda *s: pl.BlockSpec(s, lambda t: (0,) * len(s), pipeline_mode=pl.Buffered(1))
            outs = [jax.ShapeDtypeStruct((d, part), BF16)] * 2 + [jax.ShapeDtypeStruct((part, d), BF16)]
            out_specs = [whole(d, part)] * 2 + [whole(part, d)]
            if keep:
                outs += [jax.ShapeDtypeStruct((every, part), BF16)] * 2
                out_specs += [tile(part)] * 2
            return run(
                "by_hidden",
                next(cid),
                compute,
                (n_steps,),
                [by_h, w.reshape(chips, PARTS, share, d), gate, up, a],
                [tile(d), pl.BlockSpec((chips, 1, share, d), lambda t: (0, p, 0, 0), pipeline_mode=pl.Buffered(1)), piece, piece, tile(d)],
                outs,
                out_specs,
                [pltpu.VMEM((d, part), F32)] * 2 + [pltpu.VMEM((part, d), F32)],
                comms=comms,
                flops=4 * unit // PARTS,
            )

        def by_input(by_gates, by_ups, wg, wu, h, by_h, comms=()):
            def terms(lhs, rhs):
                return sum(
                    mm_t(lhs[side * PARTS + p][...], rhs[side][:, p * part : (p + 1) * part]) for side in range(2) for p in range(PARTS)
                )

            def finish(total, h, by_h):
                return (by_h + by_normed(h, total.astype(BF16)),)

            lhs = [*by_gates, *by_ups]
            (by_hs,), got = over_cores("by_input", terms, lhs, [swapped(part)] * len(lhs), [wg, wu], [h, by_h], finish, 0, comms)
            return by_hs, got

        def just(comm):
            def compute(*_):
                pass

            return run("gather", next(cid), compute, (1,), [], [], [], [], comms=[comm])[1]

        flat = lambda w: w.reshape(-1, w.shape[-1])
        h0 = x[0]
        a0 = normed(both(h0))
        dys = both(dy[0])
        (wg0,) = just(Gather(blocks[0, 0]))
        gate0, wu0 = gate_of(a0, flat(wg0), blocks[1, 0])
        up0, hidden0, wd0 = up_of(a0, flat(wu0), gate0, blocks[2, 0])
        h1, a1, wg1 = down_of(hidden0, wd0, h0, blocks[0, 1])
        gate1, wu1 = gate_of(a1, flat(wg1), blocks[1, 1])
        up1, hidden1, wd1 = up_of(a1, flat(wu1), gate1, blocks[2, 1])

        pending, mine = None, {}

        def scatters():
            if pending is None:
                return []
            return [Scatter(g.reshape(8, -1, g.shape[-1])) for g in pending[1]]

        def settle(got):
            if pending is not None:
                for i, g in enumerate(pending[1]):
                    own = lax.dynamic_index_in_dim(g.reshape(chips, -1, g.shape[-1]), chip, keepdims=False)
                    terms = [own] + [t.reshape(own.shape) for t in got[2 * i : 2 * i + 2]]
                    mine[pending[0] + (i,)] = sum(t.astype(F32) for t in terms).astype(BF16)

        kept = {0: (wd0, gate0, up0, a0), 1: (wd1, gate1, up1, a1)}
        by_hs = dys
        for n in (1, 0):
            by_gates, by_ups = [], []
            for p in range(PARTS):
                results, got = by_hidden(p, by_hs, *kept[n], bool(n), scatters())
                settle(got)
                pending = ((n, p), results[:3])
                by_gates += results[3:4]
                by_ups += results[4:5]
            if n:
                by_hs, got = by_input(by_gates, by_ups, flat(wg1), flat(wu1), h1, dy[0], scatters())
                settle(got)
                pending = None
        got = run("last", next(cid), lambda *_: None, (1,), [], [], [], [], comms=scatters())[1]
        settle(got)

        gradients = []
        for i in range(2):
            each = []
            for n in range(layers):
                got = jnp.concatenate([mine[n, p, i] for p in range(PARTS)], axis=1)
                top, bottom = got[:rows], got[rows:]
                each.append(join(jnp.where(first, top, bottom), sibling(jnp.where(first, bottom, top))))
            gradients.append(jnp.stack(each))
        gradients.append(jnp.stack([jnp.concatenate([mine[n, p, 2] for p in range(PARTS)]) for n in range(layers)]))
        new = [adamw(w.astype(F32), m, v, g.astype(F32)) for w, m, v, g in zip(weights, m, v, gradients, strict=True)]
        return tuple(one[which] for which in range(3) for one in new)

    states, cut = P(("rep", "dp"), None, None), P(None, "dp", None)
    return jax.shard_map(
        step,
        mesh=mesh,
        in_specs=(states, states) + (cut,) * 9,
        out_specs=(P("rep", "dp", None),) * 9,
        check_vma=False,
    )
```

time: 1010 us -> 963 us (0.953)
  Pallas kernels: 0 us -> 736 us
  matrix products: 531 us -> 0 us
  waiting for transfers between devices: 393 us -> 0.03 us
  other arithmetic: 40.3 us -> 116 us
  local copies, waits for them, and re-layouts: 26.4 us -> 95 us
  between operations: 14.8 us -> 2.13 us
    pallas_call x0 -> x14, Pallas kernels: none -> 736 us  [run(): pl.pallas_call(kernel, name=name, grid=grid, in_specs=list(in_specs) + [A...]
    dot_general x15 -> x0, matrix products: 531 us -> none  [the longest x5 185 us: layer(): up = jnp.dot(a, w['w_up'], preferred_element_type=jnp.float32)]
    reduce_scatter x6 -> x0, waiting for transfers between devices: 225 us -> none  [step(): lax.psum_scatter(by_w[name], 'dp', scatter_dimension=0, tiled=True)]
    all_gather x6 -> x0, waiting for transfers between devices: 167 us -> none  [fetched(): lax.all_gather(w[number], 'dp', axis=0, tiled=True)]
    another operation x0 -> x24, local copies, waits for them, and re-layouts: none -> 64.5 us  [the longest x4 23.1 us: split(): w.reshape(rows, chips, 2, PARTS, share)]
    convert_element_type x3 -> x22, other arithmetic: 28.3 us -> 58.3 us  [the longest x18 24.9 us: settle(): mine[pending[0] + (i,)] = sum((t.astype(F32) for t in terms)).astype(BF16)]
    select_n x0 -> x10, other arithmetic: none -> 21 us  [the longest x2 8.71 us: split(): return (jnp.where(first, even, odd), jnp.where(first, odd, even))]
    select_n x0 -> x16, local copies, waits for them, and re-layouts: none -> 20.6 us  [split(): return (jnp.where(first, even, odd), jnp.where(first, odd, even))]
  transfers between devices with their start and end apart: 12 -> 10, of which waited for: 10 -> 0; matrix products, arithmetic and copies ran while one was open for 42% -> 13% of each run, Pallas kernels for 0% -> 53%
where the time goes in v1:
time: 963 us; the launch traced here: 952 us
  Pallas kernels  736 us (76%)
  other arithmetic  116 us (12%)
  local copies, waits for them, and re-layouts  95 us (10%)
    pallas_call x14, Pallas kernels, run(): pl.pallas_call(kernel, name=name, grid=grid, in_specs=list(in_specs) + [A...  736 us
    convert_element_type x18, other arithmetic, settle(): mine[pending[0] + (i,)] = sum((t.astype(F32) for t in terms)).astype(BF16)  24.9 us
    convert_element_type x3, other arithmetic, adamw(): return ((w - 0.02 * step).astype(BF16), m, v)  24.8 us
    another operation x4, local copies, waits for them, and re-layouts, split(): w.reshape(rows, chips, 2, PARTS, share)  23.1 us
    another operation x16, local copies, waits for them, and re-layouts, join(): jnp.stack([jnp.where(first, mine, theirs), jnp.where(first, theirs, mine)])  22.9 us
    select_n x16, local copies, waits for them, and re-layouts, split(): return (jnp.where(first, even, odd), jnp.where(first, odd, even))  20.6 us
  transfers between devices with their start and end apart: 10, of which 0 were waited for; matrix products, arithmetic and copies ran while one was open for 13% of the time, Pallas kernels for 53%

profile of v1, /device:TPU:0, one launch (start us, length us, event | category | flops | bytes accessed | tf_op | source)
XLA Modules:
  0.0 952.3 jit_solution(9880638062310663468)
XLA Ops:
  0.7 3.4 fusion.43
  4.1 6.1 reshape_squeeze.18
  11.8 6.1 reshape_squeeze.19
  17.9 4.4 broadcast_select_fusion.5
  25.2 4.9 reshape_squeeze.21
  30.2 6.0 reshape_squeeze.22
  36.1 4.3 broadcast_select_fusion.1
  43.8 3.1 select_n.209
  51.3 1.7 fusion.41
  53.0 1.8 copy.34
  64.2 47.9 %gather.1 = bf16[8,144,2304]{2,1,0:T(8,128)(2,1)} custom-call(bf16[2,144,2304]{2,1,0:T(8,128)(2,1)} %pad_maximum_fusion.5.refs_0_), custom_call_target="tpu_custom_call" | custom-call | tf_op jit(solution)/shard_map/gather/pallas_call | solution.py:198
  119.7 4.2 fusion
  124.0 8.7 fusion.1.refs_0_.refs_4_
  132.6 48.9 %gate.2 = (f32[4096,2304]{1,0:T(8,128)}, bf16[8,144,2304]{2,1,0:T(8,128)(2,1)}) custom-call(bf16[4096,1152]{1,0:T(8,128)(2,1)} %fusion.1.refs_0_.refs_4_, bf16[1152,2304]{1,0:T(8,128)(2,1)} %bitcast.252, bf16[2,144,2304]{2,1,0:T(8,128)(2,1)} %pad_maximum_fusion.6.refs_2_), custom_call_target="tpu_custom_call" | custom-call | flops 21743271936 | tf_op jit(solution)/shard_map/gate/pallas_call | solution.py:198
  181.6 53.5 %up.2 = (f32[4096,2304]{1,0:T(8,128)}, bf16[4096,2304]{1,0:T(8,128)(2,1)}, bf16[8,288,1152]{2,1,0:T(8,128)(2,1)}) custom-call(bf16[4096,1152]{1,0:T(8,128)(2,1)} %fusion.1.refs_0_.refs_4_, bf16[1152,2304]{1,0:T(8,128)(2,1)} %bitcast.317, f32[4096,2304]{1,0:T(8,128)} %get-tuple-element.83.refs_2_, bf16[2,288,1152]{2,1,0:T(8,128)(2,1)} %bitcast.267), custom_call_target="tpu_custom_call" | custom-call | flops 21743271936 | tf_op jit(solution)/shard_map/up/pallas_call | solution.py:198
  235.1 50.5 %down.1 = (bf16[2048,1152]{1,0:T(8,128)(2,1)}, bf16[2,2048,1152]{2,1,0:T(8,128)(2,1)}, bf16[8,144,2304]{2,1,0:T(8,128)(2,1)}) custom-call(bf16[4096,2304]{1,0:T(8,128)(2,1)} %get-tuple-element.84.refs_0_, bf16[4,3,192,1152]{3,2,1,0:T(8,128)(2,1)} %bitcast.306, bf16[2048,1152]{1,0:T(8,128)(2,1)} %bitcast.243, bf16[2,144,2304]{2,1,0:T(8,128)(2,1)} %pad_maximum_fusion.7.refs_3_), custom_call_target="tpu_custom_call" | custom-call | flops 21743271936 | tf_op jit(solution)/shard_map/down/pallas_call | solution.py:198
  285.6 48.8 %gate.3 = (f32[4096,2304]{1,0:T(8,128)}, bf16[8,144,2304]{2,1,0:T(8,128)(2,1)}) custom-call(bf16[4096,1152]{1,0:T(8,128)(2,1)} %bitcast.301, bf16[1152,2304]{1,0:T(8,128)(2,1)} %bitcast.310, bf16[2,144,2304]{2,1,0:T(8,128)(2,1)} %pad_maximum_fusion.8.refs_2_), custom_call_target="tpu_custom_call" | custom-call | flops 21743271936 | tf_op jit(solution)/shard_map/gate/pallas_call | solution.py:198
  334.4 53.3 %up.3 = (f32[4096,2304]{1,0:T(8,128)}, bf16[4096,2304]{1,0:T(8,128)(2,1)}, bf16[8,288,1152]{2,1,0:T(8,128)(2,1)}) custom-call(bf16[4096,1152]{1,0:T(8,128)(2,1)} %bitcast.302, bf16[1152,2304]{1,0:T(8,128)(2,1)} %bitcast.312, f32[4096,2304]{1,0:T(8,128)} %get-tuple-element.89.refs_2_, bf16[2,288,1152]{2,1,0:T(8,128)(2,1)} %bitcast.266), custom_call_target="tpu_custom_call" | custom-call | flops 21743271936 | tf_op jit(solution)/shard_map/up/pallas_call | solution.py:198
  387.7 9.8 %pad_maximum_fusion.refs_0_ = bf16[4096,1152]{1,0:T(8,128)(2,1)} fusion(bf16[2048,1152]{1,0:T(8,128)(2,1)} %collective-permute-done, bf16[2048,1152]{1,0:T(8,128)(2,1)} %bitcast.258), kind=kLoop, calls=%fused_computation.4 | loop fusion | flops 18874368 | bytes 18874368 | tf_op jit(solution)/shard_map/concatenate | solution.py:252
  397.4 49.9 %by_hidden.6 = (bf16[1152,768]{1,0:T(8,128)(2,1)}, bf16[1152,768]{1,0:T(8,128)(2,1)}, bf16[768,1152]{1,0:T(8,128)(2,1)}, bf16[4096,768]{1,0:T(8,128)(2,1)}, bf16[4096,768]{1,0:T(8,128)(2,1)}) custom-call(bf16[4096,1152]{1,0:T(8,128)(2,1)} %pad_maximum_fusion.refs_0_, bf16[4,3,192,1152]{3,2,1,0:T(8,128)(2,1)} %bitcast.314, ...), custom_call_target="tpu_custom_call" | custom-call | flops 28991029248 | tf_op jit(solution)/shard_map/by_hidden/pallas_call | solution.py:198
  447.3 56.6 %by_hidden.7 = (bf16[1152,768]{1,0:T(8,128)(2,1)}, bf16[1152,768]{1,0:T(8,128)(2,1)}, bf16[768,1152]{1,0:T(8,128)(2,1)}, bf16[4096,768]{1,0:T(8,128)(2,1)}, bf16...) custom-call(bf16[4096,1152]{1,0:T(8,128)(2,1)} %pad_maximum_fusion.r, ...), custom_call_target="tpu_custom_call" | custom-call | flops 28991029248 | tf_op jit(solution)/shard_map/by_hidden/pallas_call | solution.py:198
  503.9 53.7 %by_hidden.8 = (bf16[1152,768]{1,0:T(8,128)(2,1)}, bf16[1152,768]{1,0:T(8,128)(2,1)}, bf16[768,1152]{1,0:T(8,128)(2,1)}, bf16[4096,768]{1,0:T(8,128)(2,1)}, bf16...) custom-call(bf16[4096,1152]{1,0:T(8,128)(2,1)} %pad_maximum_fusion.r, ...), custom_call_target="tpu_custom_call" | custom-call | flops 28991029248 | tf_op jit(solution)/shard_map/by_hidden/pallas_call | solution.py:198
  558.9 70.6 %by_input.1 = (bf16[2,2048,1152]{2,1,0:T(8,128)(2,1)}, bf16[2,144,768]{2,1,0:T(8,128)(2,1)}, bf16[2,144,768]{2,1,0:T(8,128)(2,1)}, bf16[2,144,768]{2,1,0:T(8,128...) custom-call(bf16[4096,768]{1,0:T(8,128)(2,1)} %get-tuple-element.92.refs_0_, ...), custom_call_target="tpu_custom_call" | custom-call | flops 130459631616 | tf_op jit(solution)/shard_map/by_input/pallas_call | solution.py:198
  639.7 49.0 %by_hidden.9 = (bf16[1152,768]{1,0:T(8,128)(2,1)}, bf16[1152,768]{1,0:T(8,128)(2,1)}, bf16[768,1152]{1,0:T(8,128)(2,1)}) custom-call(bf16[4096,1152]{1,0:T(8,128)(2,1)} %bitcast.298, bf16[4,3,192,1152]{3,2,1,0:T(8,128)(2,1)} %bitcast.307, f32[4096,2304]{1,0:T(8,128)} %get-tuple-element.83.refs_2_, f32[4096,2304]{1,0:T(8,128)} %get-tuple-element.109.refs_3_, ...), custom_call_target="tpu_custom_call" | custom-call | flops 28991029248 | tf_op jit(solution)/shard_map/by_hidden/pallas_call | solution.py:198
  688.7 56.0 %by_hidden.10 = (bf16[1152,768]{1,0:T(8,128)(2,1)}, bf16[1152,768]{1,0:T(8,128)(2,1)}, bf16[768,1152]{1,0:T(8,128)(2,1)}, bf16[2,144,768]{2,1,0:T(8,128)(2,1)}, ...) custom-call(bf16[4096,1152]{1,0:T(8,128)(2,1)} %bitcast.299, ...), custom_call_target="tpu_custom_call" | custom-call | flops 28991029248 | tf_op jit(solution)/shard_map/by_hidden/pallas_call | solution.py:198
  744.7 56.3 %by_hidden.11 = (bf16[1152,768]{1,0:T(8,128)(2,1)}, bf16[1152,768]{1,0:T(8,128)(2,1)}, bf16[768,1152]{1,0:T(8,128)(2,1)}, bf16[2,144,768]{2,1,0:T(8,128)(2,1)}, ...) custom-call(bf16[4096,1152]{1,0:T(8,128)(2,1)} %bitcast.300, ...), custom_call_target="tpu_custom_call" | custom-call | flops 28991029248 | tf_op jit(solution)/shard_map/by_hidden/pallas_call | solution.py:198
  802.5 2.2 fusion.34
  804.7 41.4 %last.1 = (bf16[2,144,768]{2,1,0:T(8,128)(2,1)}, bf16[2,144,768]{2,1,0:T(8,128)(2,1)}, bf16[2,144,768]{2,1,0:T(8,128)(2,1)}, bf16[2,144,768]{2,1,0:T(8,128)(2,1)...) custom-call(bf16[8,144,768]{2,1,0:T(8,128)(2,1)} %bitcast.264, bf16[8,144,768]{2,1,0:T(8,128)(2,1)} %bitcast.262, ...), custom_call_target="tpu_custom_call" | custom-call | tf_op jit(solution)/shard_map/last/pallas_call | solution.py:198
  864.4 6.3 fusion.12
  870.7 2.3 broadcast_select_fusion.17
  873.0 2.3 broadcast_select_fusion.9
  875.2 2.4 stack.102
  878.2 2.4 stack.109
  882.2 2.6 stack.110
  886.1 3.1 maximum_bitcast_fusion.3
  889.2 5.1 stack_reshape.15
  894.2 2.4 stack.103
  897.2 3.1 maximum_bitcast_fusion.1
  900.3 5.2 stack_reshape.13
  905.5 2.0 broadcast_select_fusion.13
  908.9 2.0 broadcast_select_fusion.21
  911.0 2.7 stack.99
  919.0 3.0 stack_reshape.12
  921.9 2.4 stack.107
  924.9 3.1 maximum_bitcast_fusion.2
  928.0 5.2 stack_reshape.14
  933.3 9.8 %fusion.8 = (bf16[2,144,4608]{2,1,0:T(8,128)(2,1)}, f32[2,144,4608]{2,1,0:T(8,128)}, f32[2,144,4608]{2,1,0:T(8,128)}) fusion(bf16[2,144,4608]{2,1,0:T(8,128)(2,1)S(1)} %copy-done.7, bf16[1,144,4608]{2,1,0:T(8,128)(2,1)} %stack_reshape.15, bf16[1,144,4608]{2,1,0:T(8,128)(2,1)} %stack_reshape.14, f32[2,144,4608]{2,1,0:T(8,128)} %param.20, ...), kind=kLoop, calls=%fused_computation.24 | loop fusion | flops 25214976 | bytes 29196288 | tf_op jit(solution)/shard_map/convert_element_type | solution.py:46
  943.0 8.8 fusion.4
  (193 shorter events, 71.0 us)
Async XLA Ops:
  4.0 6.1 copy-start.6
  11.8 6.1 copy-start.9
  24.4 37.4 %collective-permute-start.2 = (bf16[144,2304]{1,0:T(8,128)(2,1)}, bf16[144,2304]{1,0:T(8,128)(2,1)}, u32[]{:S(2)}, u32[]{:S(2)}) collective-permute-start(bf16[144,2304]{1,0:T(8,128)(2,1)} %select_n.197), channel_id=1, source_target_pairs={{0,1},{1,0},{2,3},{3,2},{4,5},{5,4},{6,7},{7,6}} | collective-permute-start | bytes 1990664 | tf_op jit(solution)/shard_map/ppermute | solution.py:218
  42.5 69.6 %collective-permute-start.5 = (bf16[144,2304]{1,0:T(8,128)(2,1)}, bf16[144,2304]{1,0:T(8,128)(2,1)}, u32[]{:S(2)}, u32[]{:S(2)}) collective-permute-start(bf16[144,2304]{1,0:T(8,128)(2,1)} %select_n.215), channel_id=1, source_target_pairs={{0,1},{1,0},{2,3},{3,2},{4,5},{5,4},{6,7},{7,6}} | collective-permute-start | bytes 1990664 | tf_op jit(solution)/shard_map/ppermute | solution.py:218
  43.8 7.5 copy-start.4
  47.0 66.4 %collective-permute-start.4 = (bf16[144,2304]{1,0:T(8,128)(2,1)}, bf16[144,2304]{1,0:T(8,128)(2,1)}, u32[]{:S(2)}, u32[]{:S(2)}) collective-permute-start(bf16[144,2304]{1,0:T(8,128)(2,1)} %select_n.209), channel_id=1, source_target_pairs={{0,1},{1,0},{2,3},{3,2},{4,5},{5,4},{6,7},{7,6}} | collective-permute-start | bytes 1990664 | tf_op jit(solution)/shard_map/ppermute | solution.py:218
  50.8 66.2 %collective-permute-start.3 = (bf16[144,2304]{1,0:T(8,128)(2,1)}, bf16[144,2304]{1,0:T(8,128)(2,1)}, u32[]{:S(2)}, u32[]{:S(2)}) collective-permute-start(bf16[144,2304]{1,0:T(8,128)(2,1)} %select_n.203), channel_id=1, source_target_pairs={{0,1},{1,0},{2,3},{3,2},{4,5},{5,4},{6,7},{7,6}} | collective-permute-start | bytes 1990664 | tf_op jit(solution)/shard_map/ppermute | solution.py:218
  50.8 68.9 %collective-permute-start.1 = (bf16[2048,1152]{1,0:T(8,128)(2,1)}, bf16[2048,1152]{1,0:T(8,128)(2,1)}, u32[]{:S(2)}, u32[]{:S(2)}) collective-permute-start(bf16[2048,1152]{1,0:T(8,128)(2,1)} %bitcast.242), channel_id=1, source_target_pairs={{0,1},{1,0},{2,3},{3,2},{4,5},{5,4},{6,7},{7,6}} | collective-permute-start | bytes 14155784 | tf_op jit(solution)/shard_map/ppermute | solution.py:218
  53.0 3.4 copy-start.14
  54.8 3.7 copy-start.13
  56.9 3.7 copy-start.12
  61.8 325.8 %collective-permute-start = (bf16[2048,1152]{1,0:T(8,128)(2,1)}, bf16[2048,1152]{1,0:T(8,128)(2,1)}, u32[]{:S(2)}, u32[]{:S(2)}) collective-permute-start(bf16[2048,1152]{1,0:T(8,128)(2,1)} %bitcast.257), channel_id=1, source_target_pairs={{0,1},{1,0},{2,3},{3,2},{4,5},{5,4},{6,7},{7,6}} | collective-permute-start | bytes 14155784 | tf_op jit(solution)/shard_map/ppermute | solution.py:218
  64.2 47.9 %copy-start.19 = (bf16[144,2304]{1,0:T(8,128)(2,1)S(1)}, bf16[144,2304]{1,0:T(8,128)(2,1)}, u32[]{:S(2)}) copy-start(bf16[144,2304]{1,0:T(8,128)(2,1)} %select_n.213) | copy-start | bytes 1990660
  114.7 5.0 slice-start
  115.9 3.8 slice-start.1
  503.9 53.7 %copy-start.44 = (bf16[2,144,768]{2,1,0:T(8,128)(2,1)S(1)}, bf16[2,144,768]{2,1,0:T(8,128)(2,1)}, u32[]{:S(2)}) copy-start(bf16[2,144,768]{2,1,0:T(8,128)(2,1)} %get-tuple-element.137) | copy-start | bytes 1327108
  503.9 53.7 %copy-start.45 = (bf16[2,144,768]{2,1,0:T(8,128)(2,1)S(1)}, bf16[2,144,768]{2,1,0:T(8,128)(2,1)}, u32[]{:S(2)}) copy-start(bf16[2,144,768]{2,1,0:T(8,128)(2,1)} %get-tuple-element.138) | copy-start | bytes 1327108
  558.9 72.0 %copy-start.38 = (bf16[2,144,768]{2,1,0:T(8,128)(2,1)S(1)}, bf16[2,144,768]{2,1,0:T(8,128)(2,1)}, u32[]{:S(2)}) copy-start(bf16[2,144,768]{2,1,0:T(8,128)(2,1)} %get-tuple-element.139) | copy-start | bytes 1327108
  558.9 72.0 %copy-start.39 = (bf16[2,144,768]{2,1,0:T(8,128)(2,1)S(1)}, bf16[2,144,768]{2,1,0:T(8,128)(2,1)}, u32[]{:S(2)}) copy-start(bf16[2,144,768]{2,1,0:T(8,128)(2,1)} %get-tuple-element.140) | copy-start | bytes 1327108
  632.2 2.4 copy-start.42
  632.2 2.4 copy-start.43
  632.3 3.6 copy-start.34
  632.3 3.6 copy-start.35
  639.2 231.5 %collective-permute-start.7 = (bf16[144,2304]{1,0:T(8,128)(2,1)}, bf16[144,2304]{1,0:T(8,128)(2,1)}, u32[]{:S(2)}, u32[]{:S(2)}) collective-permute-start(bf16[144,2304]{1,0:T(8,128)(2,1)} %broadcast_select_fusion.18), channel_id=1, source_target_pairs={{0,1},{1,0},{2,3},{3,2},{4,5},{5,4},{6,7},{7,6}} | collective-permute-start | bytes 1990664 | tf_op jit(solution)/shard_map/ppermute | solution.py:218
  639.5 233.4 %collective-permute-start.9 = (bf16[144,2304]{1,0:T(8,128)(2,1)}, bf16[144,2304]{1,0:T(8,128)(2,1)}, u32[]{:S(2)}, u32[]{:S(2)}) collective-permute-start(bf16[144,2304]{1,0:T(8,128)(2,1)} %broadcast_select_fusion.10), channel_id=1, source_target_pairs={{0,1},{1,0},{2,3},{3,2},{4,5},{5,4},{6,7},{7,6}} | collective-permute-start | bytes 1990664 | tf_op jit(solution)/shard_map/ppermute | solution.py:218
  847.6 3.4 copy-start.40
  847.6 3.4 copy-start.41
  848.9 3.5 copy-start.46
  848.9 3.5 copy-start.47
  851.0 5.9 copy-start.24
  851.1 5.9 copy-start.25
  851.1 7.2 copy-start.23
  852.4 11.7 %slice-start.4 = ((s8[5308416]{0:T(1024)(128)(4,1)}), s8[4194304]{0:T(1024)(128)(4,1)S(1)}, s32[]{:S(2)}) async-start(s8[5308416]{0:T(1024)(128)(4,1)} %bitcast.255), calls=%async_computation.4 | async-start | bytes 8388608
  853.9 4.3 copy-start.2
  854.0 4.3 copy-start.22
  854.0 10.1 %slice-start.2 = ((s8[5308416]{0:T(1024)(128)(4,1)}), s8[4194304]{0:T(1024)(128)(4,1)S(1)}, s32[]{:S(2)}) async-start(s8[5308416]{0:T(1024)(128)(4,1)} %bitcast.253), calls=%async_computation.2 | async-start | bytes 8388608
  854.9 50.6 %collective-permute-start.8 = (bf16[144,2304]{1,0:T(8,128)(2,1)}, bf16[144,2304]{1,0:T(8,128)(2,1)}, u32[]{:S(2)}, u32[]{:S(2)}) collective-permute-start(bf16[144,2304]{1,0:T(8,128)(2,1)} %broadcast_select_fusion.14), channel_id=1, source_target_pairs={{0,1},{1,0},{2,3},{3,2},{4,5},{5,4},{6,7},{7,6}} | collective-permute-start | bytes 1990664 | tf_op jit(solution)/shard_map/ppermute | solution.py:218
  854.9 54.0 %collective-permute-start.6 = (bf16[144,2304]{1,0:T(8,128)(2,1)}, bf16[144,2304]{1,0:T(8,128)(2,1)}, u32[]{:S(2)}, u32[]{:S(2)}) collective-permute-start(bf16[144,2304]{1,0:T(8,128)(2,1)} %broadcast_select_fusion.22), channel_id=1, source_target_pairs={{0,1},{1,0},{2,3},{3,2},{4,5},{5,4},{6,7},{7,6}} | collective-permute-start | bytes 1990664 | tf_op jit(solution)/shard_map/ppermute | solution.py:218
  858.3 5.8 slice-start.5
  859.7 2.8 copy-start.30
  859.7 2.8 copy-start.31
  859.7 4.4 slice-start.3
  864.4 6.3 copy-start.1
  900.3 5.2 copy-start.3
  928.0 5.3 copy-start.7
  933.2 9.8 %copy-start.8 = (bf16[2,144,4608]{2,1,0:T(8,128)(2,1)S(1)}, bf16[2,144,4608]{2,1,0:T(8,128)(2,1)}, u32[]{:S(2)}) copy-start(bf16[2,144,4608]{2,1,0:T(8,128)(2,1)} %param.13) | copy-start | bytes 7962628
  933.2 9.8 %copy-start.10 = (bf16[1,144,4608]{2,1,0:T(8,128)(2,1)S(1)}, bf16[1,144,4608]{2,1,0:T(8,128)(2,1)}, u32[]{:S(2)}) copy-start(bf16[1,144,4608]{2,1,0:T(8,128)(2,1)} %stack_reshape.13) | copy-start | bytes 3981316
  933.2 9.8 %copy-start.11 = (bf16[1,144,4608]{2,1,0:T(8,128)(2,1)S(1)}, bf16[1,144,4608]{2,1,0:T(8,128)(2,1)}, u32[]{:S(2)}) copy-start(bf16[1,144,4608]{2,1,0:T(8,128)(2,1)} %stack_reshape.12) | copy-start | bytes 3981316
  (16 other events, 25.4 us)

commit v2 on v1

v2 whole, which is shorter than its diff:
```python
import functools
import math

import jax
import jax.numpy as jnp
from jax import lax
from jax.experimental import pallas as pl
from jax.experimental.pallas import tpu as pltpu
from jax.sharding import PartitionSpec as P

F32, BF16 = jnp.float32, jnp.bfloat16
MESH = pl.DeviceIdType.MESH
ANY = pl.BlockSpec(memory_space=pl.ANY)
PARTS = 3
TILE = 512


def mm(a, w):
    return lax.dot_general(a, w, (((1,), (0,)), ((), ())), preferred_element_type=F32)


def mm_t(a, w):
    return lax.dot_general(a, w, (((1,), (1,)), ((), ())), preferred_element_type=F32)


def t_mm(a, d):
    return lax.dot_general(a, d, (((0,), (0,)), ((), ())), preferred_element_type=F32)


def normed(h):
    wide = h.astype(F32)
    scale = lax.rsqrt(jnp.mean(wide**2, -1, keepdims=True) + 1e-6)
    return (wide * scale).astype(BF16)


def by_normed(h, by_a):
    wide, by = h.astype(F32), by_a.astype(F32)
    scale = lax.rsqrt(jnp.mean(wide**2, -1, keepdims=True) + 1e-6)
    return (scale * by - wide * (scale**3 * jnp.mean(wide * by, -1, keepdims=True))).astype(BF16)


def adamw(w, m, v, g):
    m = 0.9 * m + 0.1 * g
    v = 0.95 * v + 0.05 * g * g
    step = m * lax.rsqrt(v + 1e-8) + 0.1 * w
    return (w - 0.02 * step).astype(BF16), m, v


def other(me, bit):
    return me + bit - 2 * bit * ((me // bit) % 2)


def remote(src, dst, sems, n, bit):
    return pltpu.make_async_remote_copy(
        src_ref=src,
        dst_ref=dst,
        send_sem=sems[0].at[n],
        recv_sem=sems[1].at[n],
        device_id={"dp": other(lax.axis_index("dp"), bit)},
        device_id_type=MESH,
    )


class Gather:
    bits = (2, 4)

    def __init__(self, block, source=None, index=None):
        _, r, n = block.shape[-3:]
        self.source = source
        self.index = index
        self.ins = [] if source else [block]
        self.outs = [jax.ShapeDtypeStruct((8, r, n), block.dtype)]
        self.scratch = [pltpu.VMEM((2, r, n), block.dtype), pltpu.SemaphoreType.DMA((2,)), pltpu.SemaphoreType.DMA((6,)), pltpu.SemaphoreType.DMA((6,))]

    def bind(self, ins, outs, scratch, own):
        (full,), (held, local, *sems) = outs, scratch
        block = self.source(own) if self.source else ins[0] if self.index is None else ins[0].at[self.index]
        chip = lax.axis_index("dp") // 2
        at = lambda bit, half: full.at[other(chip, bit) * 2 + half] if bit else full.at[chip * 2 + half]
        self.copies = [
            remote(block.at[1], at(0, 1), sems, 0, 2),
            remote(block.at[0], at(0, 0), sems, 1, 4),
            remote(block.at[0], at(0, 0), sems, 2, 2),
            remote(block.at[1], at(0, 1), sems, 3, 4),
            remote(at(2, 0), at(2, 0), sems, 4, 2),
            remote(at(1, 1), at(1, 1), sems, 5, 4),
        ]
        self.own = [pltpu.make_async_copy(block, held, local.at[0]), pltpu.make_async_copy(held, full.at[pl.ds(chip * 2, 2)], local.at[1])]

    def begin(self):
        for copy in (*self.copies[:2], self.own[0]):
            copy.start()

    def more(self):
        for copy in self.copies[2:4]:
            copy.start()

    def middle(self):
        self.own[0].wait()
        self.own[1].start()
        self.copies[1].wait_recv()
        self.copies[4].start()
        self.copies[0].wait_recv()
        self.copies[5].start()

    def late(self):
        pass

    def end(self):
        for n in (2, 3, 4, 5):
            self.copies[n].wait_recv()

    def finish(self):
        pass

    def close(self):
        for copy in self.copies:
            copy.wait_send()
        self.own[1].wait()


class Scatter:
    bits = (1, 2, 4)

    def __init__(self, blocks, rows):
        _, r, n = blocks.shape
        self.ins, self.rows = [blocks], rows
        self.outs = [jax.ShapeDtypeStruct((r, n), BF16)] * 2 if rows else [jax.ShapeDtypeStruct((2, r, n), BF16)]
        self.scratch = [pltpu.VMEM((2, r, n), BF16)] * 6 + [pltpu.SemaphoreType.DMA((4,))] + [pltpu.SemaphoreType.DMA((7,))] * 2

    def bind(self, ins, outs, scratch, own):
        (blocks,), (came, mine, total, by_y, by_x, held, local, *sems) = ins, scratch
        core, chip = lax.axis_index("dp") % 2, lax.axis_index("dp") // 2
        at = lambda bit, half: blocks.at[other(chip, bit) * 2 + half]
        diagonal = lambda half: blocks.at[(3 - chip) * 2 + half]
        self.came, self.mine, self.total, self.by_y, self.by_x, self.held = came, mine, total, by_y, by_x, held
        self.copies = [
            remote(diagonal(0), came.at[0], sems, 0, 4),
            remote(diagonal(1), came.at[1], sems, 1, 2),
            remote(at(2, 0), by_x.at[0], sems, 2, 4),
            remote(at(1, 1), by_y.at[1], sems, 3, 2),
            remote(total.at[0], by_y.at[0], sems, 4, 2),
            remote(total.at[1], by_x.at[1], sems, 5, 4),
        ]
        self.own = [pltpu.make_async_copy(at(1, 0), mine.at[0], local.at[0]), pltpu.make_async_copy(at(2, 1), mine.at[1], local.at[1])]
        self.own += [pltpu.make_async_copy(blocks.at[pl.ds(chip * 2, 2)], held, local.at[2])]
        if self.rows:
            self.out = pltpu.make_async_copy(held.at[core], outs[0], local.at[3])
            self.tell = remote(held.at[1 - core], outs[1], sems, 6, 1)
        else:
            self.out = pltpu.make_async_copy(held, outs[0], local.at[3])

    def begin(self):
        for copy in (*self.copies[:2], *self.own):
            copy.start()

    def more(self):
        for copy in self.copies[2:4]:
            copy.start()

    def middle(self):
        for half in range(2):
            self.copies[half].wait_recv()
            self.own[half].wait()
            self.total[half] = (self.came[half].astype(F32) + self.mine[half].astype(F32)).astype(BF16)

    def late(self):
        self.copies[4].start()
        self.copies[5].start()

    def end(self):
        for n in (2, 3, 4, 5):
            self.copies[n].wait_recv()
        self.own[2].wait()
        self.held[...] = (self.held[...].astype(F32) + self.by_y[...].astype(F32) + self.by_x[...].astype(F32)).astype(BF16)

    def finish(self):
        self.out.start()
        if self.rows:
            self.tell.start()

    def close(self):
        for copy in self.copies:
            copy.wait_send()
        self.out.wait()
        if self.rows:
            self.tell.wait()


def run(name, cid, compute, grid, ins, in_specs, outs, out_specs, scratch=(), comms=(), bits=(), when=(0.4, 0.5), flops=0, start=0):
    steps = math.prod(grid)
    bits = sorted(set(bits).union(*(comm.bits for comm in comms)))
    middle, late = (min(steps - 1, int(steps * w)) for w in when)
    counts = [len(ins)] + [len(c.ins) for c in comms] + [len(outs)] + [len(c.outs) for c in comms] + [len(scratch)] + [len(c.scratch) for c in comms]

    def kernel(*refs):
        refs, groups = list(refs), []
        for count in counts:
            groups.append(refs[:count])
            refs = refs[count:]
        step = 0
        for axis, size in enumerate(grid):
            step = step * size + pl.program_id(axis)
        k = len(comms) + 1
        own = groups[0], groups[k], groups[2 * k]
        for n, comm in enumerate(comms):
            comm.bind(groups[1 + n], groups[k + 1 + n], groups[2 * k + 1 + n], own)

        def do(*names):
            for what in names:
                for comm in comms:
                    getattr(comm, what)()

        @pl.when(step == 0)
        def _():
            if bits:
                barrier = pltpu.get_barrier_semaphore()
                for bit in bits:
                    pl.semaphore_signal(barrier, inc=1, device_id={"dp": other(lax.axis_index("dp"), bit)}, device_id_type=MESH)
                pl.semaphore_wait(barrier, len(bits))
            if not start:
                do("begin", "more")

        compute(*own)
        for at, what in ((start, ("begin", "more")), (middle, ("middle",)), (late, ("late",)), (steps - 1, ("end", "finish", "close"))):
            if comms and (start or at or what[0] != "begin"):

                @pl.when(step == at)
                def _():
                    do(*what)

    params = dict(collective_id=cid, has_side_effects=True) if bits else {}
    results = pl.pallas_call(
        kernel,
        name=name,
        grid=grid,
        in_specs=list(in_specs) + [ANY for c in comms for _ in c.ins],
        out_specs=list(out_specs) + [ANY for c in comms for _ in c.outs],
        out_shape=list(outs) + [o for c in comms for o in c.outs],
        scratch_shapes=list(scratch) + [s for c in comms for s in c.scratch],
        compiler_params=pltpu.CompilerParams(dimension_semantics=("arbitrary",) * len(grid), vmem_limit_bytes=62 * 2**20, **params),
        cost_estimate=pl.CostEstimate(flops=int(flops), bytes_accessed=0, transcendentals=0),
    )(*ins, *[a for c in comms for a in c.ins])
    results, got = results[: len(outs)], list(results[len(outs) :])
    return results, [[got.pop(0) for _ in comm.outs] for comm in comms]


def solution(mesh):
    size = mesh.shape["dp"]
    chips = size // 2

    def step(x, dy, *arrays):
        weights, m, v = (arrays[i : i + 3] for i in (0, 3, 6))
        layers, rows, ff = weights[0].shape
        d = rows * size
        half = ff // 2
        part = half // PARTS
        share = part // chips
        tokens = x.shape[1]
        every = 2 * tokens
        unit = 2 * every * d * half

        segments = lambda core: [(c * 2 * PARTS * share + core * PARTS * share + p * share, p * part + c * share) for p in range(PARTS) for c in range(chips)]

        cid = iter(range(100))
        wide = every // 4
        col, row = lambda n: pl.BlockSpec((wide, n), lambda j, i: (i, 0)), pl.BlockSpec((wide, part), lambda j, i: (i, j))
        weight = pl.BlockSpec((d, part), lambda j, i: (0, j))
        f32_rows, bf16_rows = jax.ShapeDtypeStruct((every, half), F32), jax.ShapeDtypeStruct((every, half), BF16)

        def gate_of(a, w, fetch):
            def compute(ins, outs, _):
                outs[0][...] = mm(ins[0][...], ins[1][...])

            (gate,), ((got,),) = run("gate", next(cid), compute, (PARTS, 4), [a, w], [col(d), weight], [f32_rows], [row], comms=[fetch], flops=unit)
            return gate, got

        def up_of(a, w, gate, fetch):
            def compute(ins, outs, _):
                up, gate = mm(ins[0][...], ins[1][...]), ins[2][...]
                outs[0][...] = up
                outs[1][...] = (jax.nn.silu(gate) * up).astype(BF16)

            tile = lambda n: pl.BlockSpec((TILE, n), lambda t: (t, 0))
            whole = pl.BlockSpec((d, half), lambda t: (0, 0), pipeline_mode=pl.Buffered(1))
            (up, hidden), ((got,),) = run(
                "up",
                next(cid),
                compute,
                (every // TILE,),
                [a, w, gate],
                [tile(d), whole, tile(half)],
                [f32_rows, bf16_rows],
                [tile(half)] * 2,
                comms=[fetch],
                flops=unit,
            )
            return up, hidden, got

        def over_cores(name, terms, lhs, lhs_specs, rhs, given, finish, keep, comms):
            tiles = tokens // TILE
            here = pl.BlockSpec((TILE, d), lambda t: (jnp.maximum(t - tiles, 0), 0))

            def compute(ins, outs, scratch):
                sent, came, state, ssem, rsem, ssem2, rsem2, local = scratch
                t = pl.program_id(0)
                product = lambda: terms(ins[: len(lhs)], ins[len(lhs) : len(lhs) + len(rhs)])
                away = lambda n: remote(sent.at[n], came.at[n], (ssem, rsem), n, 1)
                shared = outs[-1]
                rows_of = lambda n: pl.ds(pl.multiple_of(n * TILE, TILE), TILE)
                tell = lambda n: remote(state.at[n], shared.at[1, rows_of(n)], (ssem2, rsem2), n, 1)
                save = lambda n: pltpu.make_async_copy(state.at[n], shared.at[0, rows_of(n)], local.at[n])
                n = t - tiles

                @pl.when((t > 0) & (t <= tiles))
                def _():
                    away(t - 1).start()

                @pl.when(n > 0)
                def _():
                    tell(n - 1).start()
                    save(n - 1).start()

                @pl.when(t < tiles)
                def _():
                    sent[t] = product()

                @pl.when(n >= 0)
                def _():
                    away(n).wait_recv()
                    results = finish(product() + came[n], *[g[...] for g in ins[len(lhs) + len(rhs) :]])
                    for out, result in zip(outs[:-1], results[:-1], strict=True):
                        out[...] = result
                    state[n] = results[-1]

                @pl.when(n == tiles - 1)
                def _():
                    tell(tiles - 1).start()
                    save(tiles - 1).start()
                    for n in range(tiles):
                        away(n).wait_send()
                        tell(n).wait()
                        save(n).wait()

            scratch = [pltpu.VMEM((tiles, TILE, d), F32)] * 2 + [pltpu.VMEM((tiles, TILE, d), BF16)] + [pltpu.SemaphoreType.DMA((tiles,))] * 5
            whole = lambda a: pl.BlockSpec(a.shape, lambda t: (0,) * a.ndim, pipeline_mode=pl.Buffered(1))
            results, got = run(
                name,
                next(cid),
                compute,
                (2 * tiles,),
                [*lhs, *rhs, *given],
                list(lhs_specs) + [whole(a) for a in rhs] + [here] * len(given),
                [jax.ShapeDtypeStruct((tokens, d), BF16)] * keep + [jax.ShapeDtypeStruct((2, tokens, d), BF16)],
                [here] * keep + [ANY],
                scratch,
                comms=comms,
                bits=(1,),
                flops=unit * len(lhs),
            )
            return [*results[:-1], results[-1].reshape(every, d)], got

        swapped = lambda n: pl.BlockSpec((TILE, n), lambda t: ((t + tokens // TILE) % (every // TILE), 0))

        def down_of(hidden, w, h, fetches):
            def terms(lhs, rhs):
                return sum(mm(lhs[0][:, p * part : (p + 1) * part], rhs[0][:, p].reshape(part, d)) for p in range(PARTS))

            def finish(total, h):
                h = h + total.astype(BF16)
                return h, normed(h)

            (h, a), got = over_cores("down", terms, [hidden], [swapped(half)], [w.reshape(chips, PARTS, share, d)], [h], finish, 1, fetches)
            return h, a, got

        def by_hidden(by_h, a, given, given_specs, start, keep, comms=()):
            n_steps = every // TILE

            def compute(ins, outs, scratch):
                t = pl.program_id(0)

                @pl.when(t == 0)
                def _():
                    for acc in scratch:
                        acc[...] = jnp.zeros_like(acc)

                by_h, a = ins[0][...], ins[1][...]
                gate, up, by = start(by_h, a, *[r[...] for r in ins[2:]])
                sig = 1 / (1 + jnp.exp(-gate))
                act = gate * sig
                by_up = (by * act).astype(BF16)
                by_gate = (by * up * (sig * (1 + gate * (1 - sig)))).astype(BF16)
                hidden = (act * up).astype(BF16)
                if keep:
                    outs[3][...], outs[4][...] = by_gate, by_up
                for acc, lhs, rhs in zip(scratch, (a, a, hidden), (by_gate, by_up, by_h), strict=True):
                    acc[...] += t_mm(lhs, rhs)

                @pl.when(t == n_steps - 1)
                def _():
                    for acc, out in zip(scratch, outs[:3], strict=True):
                        out[...] = acc[...].astype(BF16)

            tile = lambda n: pl.BlockSpec((TILE, n), lambda t: (t, 0))
            outs = [jax.ShapeDtypeStruct((d, part), BF16)] * 2 + [jax.ShapeDtypeStruct((part, d), BF16)]
            out_specs = [whole(d, part)] * 2 + [whole(part, d)]
            if keep:
                outs += [jax.ShapeDtypeStruct((every, part), BF16)] * 2
                out_specs += [tile(part)] * 2
            return run(
                "by_hidden",
                next(cid),
                compute,
                (n_steps,),
                [by_h, a, *given],
                [tile(d), tile(d), *given_specs],
                outs,
                out_specs,
                [pltpu.VMEM((d, part), F32)] * 2 + [pltpu.VMEM((part, d), F32)],
                comms=comms,
                flops=(6 if keep else 4) * unit // PARTS,
            )

        whole = lambda *s: pl.BlockSpec(s, lambda t: (0,) * len(s), pipeline_mode=pl.Buffered(1))

        def by_last(by_h, a, wg, wu, wd, comms):
            def start(by_h, a, wg, wu, wd):
                return mm(a, wg), mm(a, wu), mm_t(by_h, wd).astype(BF16).astype(F32)

            return by_hidden(by_h, a, [wg, wu, wd], [whole(d, part)] * 2 + [whole(part, d)], start, True, comms)

        def by_first(p, by_h, a, gate, up, wd, comms):
            def start(by_h, a, gate, up, wd):
                return gate, up, mm_t(by_h, wd.reshape(part, d)).astype(BF16).astype(F32)

            piece = pl.BlockSpec((TILE, part), lambda t: (t, p))
            rows_of = pl.BlockSpec((chips, 1, share, d), lambda t: (0, p, 0, 0), pipeline_mode=pl.Buffered(1))
            return by_hidden(by_h, a, [gate, up, wd.reshape(chips, PARTS, share, d)], [piece, piece, rows_of], start, False, comms)

        def by_input(by_gates, by_ups, wg, wu, h, by_h, comms=()):
            def terms(lhs, rhs):
                return sum(
                    mm_t(each[...], w[...]) for each, w in zip(lhs, rhs, strict=True)
                )

            def finish(total, h, by_h):
                return (by_h + by_normed(h, total.astype(BF16)),)

            lhs = [*by_gates, *by_ups]
            (by_hs,), got = over_cores("by_input", terms, lhs, [swapped(part)] * len(lhs), [*wg, *wu], [h, by_h], finish, 0, comms)
            return by_hs, got

        def opened(x, dy, w_gate, w_up):
            tiles = tokens // TILE
            count = 2 * layers

            def compute(ins, outs, scratch):
                mine, give, normal, by, ssem, rsem, local, ssem2, rsem2, local2 = scratch
                *blocks, a, dys = outs
                s = pl.program_id(0)
                core = lax.axis_index("dp") % 2
                moved = lambda n: (n,) if n < 2 else range(2 + (n - 2) * PARTS, 2 + (n - 1) * PARTS)
                pieces = lambda ref, m: ref.at[m] if m < 2 else ref.at[2 + (m - 2) // PARTS, :, pl.ds((m - 2) % PARTS * part, part)]
                keep = lambda m: pltpu.make_async_copy(pieces(mine, m), blocks[m].at[core], local.at[m])
                pass_on = lambda m: remote(pieces(give, m), blocks[m].at[core], (ssem, rsem), m, 1)
                rows_of = lambda n: pl.ds(n * TILE, TILE)
                shared = lambda n: [
                    each
                    for i, (state, out) in enumerate(((normal, a), (by, dys)))
                    for each in (
                        remote(state.at[n], out.at[1, rows_of(n)], (ssem2.at[i], rsem2.at[i]), n, 1),
                        pltpu.make_async_copy(state.at[n], out.at[0, rows_of(n)], local2.at[i, n]),
                    )
                ]
                for n in range(count):
                    for k in range(2):

                        @pl.when((s == n) & (core == k))
                        def _():
                            w = ins[2 + n % 2]
                            for which, half_of in ((mine, k), (give, 1 - k)):
                                for at, to in segments(half_of):
                                    which[n, :, to : to + share] = w[0, :, at : at + share]

                    @pl.when(s == n + 1)
                    def _():
                        for m in moved(n):
                            keep(m).start()
                            pass_on(m).start()

                @pl.when(s == 2)
                def _():
                    keep(0).wait()
                    pass_on(0).wait_recv()

                for n in range(tiles):

                    @pl.when(s == count + n)
                    def _():
                        normal[n] = normed(ins[0][...])
                        by[n] = ins[1][...]

                    @pl.when(s == count + n + 1)
                    def _():
                        for copy in shared(n):
                            copy.start()

                @pl.when(s == count + tiles)
                def _():
                    pass_on(0).wait_send()
                    for m in range(1, len(blocks)):
                        keep(m).wait()
                        pass_on(m).wait()
                    for n in range(tiles):
                        for copy in shared(n):
                            copy.wait()

            tile = pl.BlockSpec((TILE, d), lambda s: (jnp.clip(s - count, 0, tiles - 1), 0))
            matrix = pl.BlockSpec((1, rows, ff), lambda s: (jnp.minimum(s // 2, layers - 1), 0, 0))
            sem = pltpu.SemaphoreType.DMA
            state = jax.ShapeDtypeStruct((2, tokens, d), BF16)
            made = [jax.ShapeDtypeStruct((2, rows, half), BF16)] * 2 + [jax.ShapeDtypeStruct((2, rows, part), BF16)] * ((count - 2) * PARTS)
            (*blocks, a, dys), ((got,),) = run(
                "open",
                next(cid),
                compute,
                (count + tiles + 1,),
                [x, dy, w_gate, w_up],
                [tile, tile, matrix, matrix],
                [*made, state, state],
                [ANY] * (len(made) + 2),
                [pltpu.VMEM((count, rows, half), BF16)] * 2
                + [pltpu.VMEM((tiles, TILE, d), BF16)] * 2
                + [sem((len(made),))] * 3
                + [sem((2, tiles))] * 3,
                comms=[Gather(jax.ShapeDtypeStruct((2, rows, half), BF16), lambda own: own[1][0])],
                bits=(1,),
                when=(0.999, 0.999),
                start=2,
            )
            return blocks, a.reshape(every, d), dys.reshape(every, d), got

        def updated(pieces):
            tile = rows // PARTS
            keys = [(n, p) for n in range(layers) for p in range(PARTS)]

            def kernel(*refs):
                state, refs = refs[:9], refs[9:]
                given, refs = refs[: 5 * len(keys)], refs[5 * len(keys) :]
                outs, scratch = refs[:9], refs[9:]
                core, layer, t = lax.axis_index("dp") % 2, pl.program_id(0), pl.program_id(1)
                for i, key in enumerate(keys):
                    gate_up, down = given[5 * i : 5 * i + 4], given[5 * i + 4]
                    for k in range(2):

                        @pl.when((core == k) & (layer == key[0]))
                        def _():
                            for which, source in enumerate(gate_up):
                                for at, to in segments(k if which % 2 == 0 else 1 - k):
                                    if to // part == key[1]:
                                        scratch[which // 2][:, at : at + share] = source[:, to % part : to % part + share].astype(F32)

                    @pl.when((layer == key[0]) & (t == key[1]))
                    def _():
                        scratch[2][...] = down[...].reshape(scratch[2].shape).astype(F32)

                for i in range(3):
                    w, m, v = (state[i + 3 * j][0] for j in range(3))
                    outs[i][0], outs[i + 3][0], outs[i + 6][0] = adamw(w.astype(F32), m, v, scratch[i][...])

            block = lambda a: pl.BlockSpec((1, a.shape[1] // PARTS, a.shape[2]), lambda n, t: (n, t, 0))
            given, given_specs = [], []
            for n, p in keys:
                given += pieces[n, p]
                given_specs += [pl.BlockSpec((tile, part), lambda k, t, n=n: (jnp.where(k == n, t, 0), 0))] * 4
                given_specs += [pl.BlockSpec(pieces[n, p][4].shape, lambda k, t: (0, 0, 0), pipeline_mode=pl.Buffered(1))]
            wide = lambda a, dtype: jax.ShapeDtypeStruct(a.shape, dtype)
            return pl.pallas_call(
                kernel,
                name="adamw",
                grid=(layers, PARTS),
                in_specs=[block(a) for a in (*weights, *m, *v)] + given_specs,
                out_specs=[block(a) for a in (*weights, *m, *v)],
                out_shape=[wide(a, BF16) for a in weights] + [wide(a, F32) for a in (*m, *v)],
                scratch_shapes=[pltpu.VMEM((a.shape[1] // PARTS, a.shape[2]), F32) for a in weights],
                compiler_params=pltpu.CompilerParams(dimension_semantics=("arbitrary",) * 2, vmem_limit_bytes=62 * 2**20),
            )(*weights, *m, *v, *given)

        flat = lambda w: w.reshape(-1, w.shape[-1])
        h0 = x[0]
        down_all = Gather(weights[2].reshape(layers, 2, -1, d), index=0)
        down_part = lambda p: Gather(weights[2].reshape(layers, PARTS, 2, -1, d), index=(1, p))
        (_, up_block, *parts), a0, dys, wg0 = opened(h0, dy[0], weights[0], weights[1])
        fetch = [[Gather(parts[p]), Gather(parts[PARTS + p]), down_part(p)] for p in range(PARTS)]
        gate0, wu0 = gate_of(a0, flat(wg0), Gather(up_block))
        up0, hidden0, wd0 = up_of(a0, flat(wu0), gate0, down_all)
        h1, a1, got = down_of(hidden0, wd0, h0, fetch[0])

        def scatters(made):
            return [Scatter(g.reshape(8, -1, g.shape[-1]), i < 2) for i, g in enumerate(made[:3])]

        full = [[flat(w) for (w,) in got]]
        made, sums = [], []
        for p in range(PARTS):
            beside = [[*fetch[1], fetch[2][0]], fetch[2][1:], []][p]
            send = [c for each in made for c in scatters(each)][[0, 0, 2][p] : [0, 2, 6][p]]
            results, got = by_last(dys, a1, *full[p], [*beside, *send])
            made.append(results)
            got_w, got_g = [flat(w) for (w,) in got[: len(beside)]], got[len(beside) :]
            sums += got_g
            if p == 0:
                full += [got_w[:3], got_w[3:]]
            if p == 1:
                full[2] += got_w
        columns = list(zip(*full, strict=True))
        by_hs, got = by_input([r[3] for r in made], [r[4] for r in made], columns[0], columns[1], h1, dy[0], scatters(made[2]))
        sums += got
        mine = {(1, p): sum(sums[3 * p : 3 * p + 3], []) for p in range(PARTS)}
        results = None
        for p in range(PARTS):
            results, got = by_first(p, by_hs, a0, gate0, up0, wd0, scatters(results) if p else [])
            if p:
                mine[0, p - 1] = sum(got, [])
        mine[0, PARTS - 1] = sum(run("last", next(cid), lambda *_: None, (1,), [], [], [], [], comms=scatters(results))[1], [])
        return tuple(updated(mine))

    states, cut = P(("rep", "dp"), None, None), P(None, "dp", None)
    return jax.shard_map(
        step,
        mesh=mesh,
        in_specs=(states, states) + (cut,) * 9,
        out_specs=(P("rep", "dp", None),) * 9,
        check_vma=False,
    )
```

time: 963 us -> 706 us (0.73)
  other arithmetic: 116 us -> 0 us
  local copies, waits for them, and re-layouts: 95 us -> 0 us
  Pallas kernels: 736 us -> 698 us
    pallas_call x14 -> x12, Pallas kernels: 736 us -> 670 us  [run(): pl.pallas_call(kernel, name=name, grid=grid, in_specs=list(in_specs) + [A...]
    another operation x24 -> x0, local copies, waits for them, and re-layouts: 64.5 us -> none  [the longest x4 23.1 us: split(): w.reshape(rows, chips, 2, PARTS, share)]
    convert_element_type x22 -> x0, other arithmetic: 58.3 us -> none  [the longest x18 24.9 us: settle(): mine[pending[0] + (i,)] = sum((t.astype(F32) for t in terms)).astype(BF16)]
    pallas_call x0 -> x1, Pallas kernels: none -> 28.5 us  [updated(): pl.pallas_call(kernel, name='adamw', grid=(layers, PARTS), in_specs=[bloc...]
    select_n x10 -> x0, other arithmetic: 21 us -> none  [the longest x2 8.71 us: split(): return (jnp.where(first, even, odd), jnp.where(first, odd, even))]
    select_n x16 -> x0, local copies, waits for them, and re-layouts: 20.6 us -> none  [split(): return (jnp.where(first, even, odd), jnp.where(first, odd, even))]
    concatenate x5 -> x0, other arithmetic: 11.2 us -> none  [the longest x1 9.75 us: both(): return jnp.concatenate([a, sibling(a)])]
    transpose x4 -> x0, other arithmetic: 10.9 us -> none  [join(): jnp.moveaxis(both.reshape(2, rows, PARTS, chips, share), (0, 2), (2, 3))]
  transfers between devices with their start and end apart: 10 -> 0, of which waited for: 0 -> 0; matrix products, arithmetic and copies ran while one was open for 13% -> 0% of each run, Pallas kernels for 53% -> 0%
where the time goes in v2:
time: 706 us; the launch traced here: 699 us
  Pallas kernels  698 us (99%)
    pallas_call x12, Pallas kernels, run(): pl.pallas_call(kernel, name=name, grid=grid, in_specs=list(in_specs) + [A...  670 us
    pallas_call x1, Pallas kernels, updated(): pl.pallas_call(kernel, name='adamw', grid=(layers, PARTS), in_specs=[bloc...  28.5 us

profile of v2, /device:TPU:0, one launch (start us, length us, event | category | flops | bytes accessed | tf_op | source)
XLA Modules:
  0.0 699.4 jit_solution(13593242009304361550)
XLA Ops:
  0.6 54.1 %open.1 = (bf16[2,144,2304]{2,1,0:T(8,128)(2,1)}, bf16[2,144,2304]{2,1,0:T(8,128)(2,1)}, bf16[2,144,768]{2,1,0:T(8,128)(2,1)}, bf16[2,144,768]{2,1,0:T(8,128)(2,...) custom-call(bf16[2048,1152]{1,0:T(8,128)(2,1)} %bitcast.38, ...), custom_call_target="tpu_custom_call" | custom-call | tf_op jit(solution)/shard_map/open/pallas_call | solution.py:233
  54.8 48.5 %gate.1 = (f32[4096,2304]{1,0:T(8,128)}, bf16[8,144,2304]{2,1,0:T(8,128)(2,1)}) custom-call(bf16[4096,1152]{1,0:T(8,128)(2,1)} %bitcast.49, bf16[1152,2304]{1,0:T(8,128)(2,1)} %bitcast.57, bf16[2,144,2304]{2,1,0:T(8,128)(2,1)} %get-tuple-element.93.refs_2_), custom_call_target="tpu_custom_call" | custom-call | flops 21743271936 | tf_op jit(solution)/shard_map/gate/pallas_call | solution.py:233
  103.3 51.0 %up.1 = (f32[4096,2304]{1,0:T(8,128)}, bf16[4096,2304]{1,0:T(8,128)(2,1)}, bf16[8,288,1152]{2,1,0:T(8,128)(2,1)}) custom-call(bf16[4096,1152]{1,0:T(8,128)(2,1)} %bitcast.50, bf16[1152,2304]{1,0:T(8,128)(2,1)} %bitcast.68, f32[4096,2304]{1,0:T(8,128)} %get-tuple-element.95.refs_2_, bf16[2,2,288,1152]{3,2,1,0:T(8,128)(2,1)} %bitcast.42), custom_call_target="tpu_custom_call" | custom-call | flops 21743271936 | tf_op jit(solution)/shard_map/up/pallas_call | solution.py:233
  154.3 51.1 %down.1 = (bf16[2048,1152]{1,0:T(8,128)(2,1)}, bf16[2,2048,1152]{2,1,0:T(8,128)(2,1)}, bf16[8,144,768]{2,1,0:T(8,128)(2,1)}, bf16[8,144,768]{2,1,0:T(8,128)(2,1)}, bf16[8,96,1152]{2,1,0:T(8,128)(2,1)}) custom-call(bf16[4096,2304]{1,0:T(8,128)(2,1)} %get-tuple-element.96.refs_0_, bf16[4,3,192,1152]{3,2,1,0:T(8,128)(2,1)} %bitcast.64, ...), custom_call_target="tpu_custom_call" | custom-call | flops 21743271936 | tf_op jit(solution)/shard_map/down/pallas_call | solution.py:233
  205.5 65.7 %by_hidden.6 = (bf16[1152,768]{1,0:T(8,128)(2,1)}, bf16[1152,768]{1,0:T(8,128)(2,1)}, bf16[768,1152]{1,0:T(8,128)(2,1)}, bf16[4096,768]{1,0:T(8,128)(2,1)}, bf16...) custom-call(bf16[4096,1152]{1,0:T(8,128)(2,1)} %bitcast.54, ...), custom_call_target="tpu_custom_call" | custom-call | flops 43486543872 | tf_op jit(solution)/shard_map/by_hidden/pallas_call | solution.py:233
  271.2 67.0 %by_hidden.7 = (bf16[1152,768]{1,0:T(8,128)(2,1)}, bf16[1152,768]{1,0:T(8,128)(2,1)}, bf16[768,1152]{1,0:T(8,128)(2,1)}, bf16[4096,768]{1,0:T(8,128)(2,1)}, bf16...) custom-call(bf16[4096,1152]{1,0:T(8,128)(2,1)} %bitcast.55, ...), custom_call_target="tpu_custom_call" | custom-call | flops 43486543872 | tf_op jit(solution)/shard_map/by_hidden/pallas_call | solution.py:233
  338.2 68.8 %by_hidden.8 = (bf16[1152,768]{1,0:T(8,128)(2,1)}, bf16[1152,768]{1,0:T(8,128)(2,1)}, bf16[768,1152]{1,0:T(8,128)(2,1)}, bf16[4096,768]{1,0:T(8,128)(2,1)}, bf16...) custom-call(bf16[4096,1152]{1,0:T(8,128)(2,1)} %bitcast.56, ...), custom_call_target="tpu_custom_call" | custom-call | flops 43486543872 | tf_op jit(solution)/shard_map/by_hidden/pallas_call | solution.py:233
  407.0 68.1 %by_input.1 = (bf16[2,2048,1152]{2,1,0:T(8,128)(2,1)}, bf16[144,768]{1,0:T(8,128)(2,1)}, bf16[144,768]{1,0:T(8,128)(2,1)}, bf16[144,768]{1,0:T(8,128)(2,1)}, bf1...) custom-call(bf16[4096,768]{1,0:T(8,128)(2,1)} %get-tuple-element.107.refs_0_, ...), custom_call_target="tpu_custom_call" | custom-call | flops 130459631616 | tf_op jit(solution)/shard_map/by_input/pallas_call | solution.py:233
  475.1 41.4 %by_hidden.9 = (bf16[1152,768]{1,0:T(8,128)(2,1)}, bf16[1152,768]{1,0:T(8,128)(2,1)}, bf16[768,1152]{1,0:T(8,128)(2,1)}) custom-call(bf16[4096,1152]{1,0:T(8,128)(2,1)} %bitcast.61, bf16[4096,1152]{1,0:T(8,128)(2,1)} %bitcast.51, f32[4096,2304]{1,0:T(8,128)} %get-tuple-element.95.refs_2_, f32[4096,2304]{1,0:T(8,128)} %get-tuple-element.131.refs_3_, ...), custom_call_target="tpu_custom_call" | custom-call | flops 28991029248 | tf_op jit(solution)/shard_map/by_hidden/pallas_call | solution.py:233
  516.5 53.0 %by_hidden.10 = (bf16[1152,768]{1,0:T(8,128)(2,1)}, bf16[1152,768]{1,0:T(8,128)(2,1)}, bf16[768,1152]{1,0:T(8,128)(2,1)}, bf16[144,768]{1,0:T(8,128)(2,1)}, bf16...) custom-call(bf16[4096,1152]{1,0:T(8,128)(2,1)} %bitcast.62, ...), custom_call_target="tpu_custom_call" | custom-call | flops 28991029248 | tf_op jit(solution)/shard_map/by_hidden/pallas_call | solution.py:233
  569.5 53.4 %by_hidden.11 = (bf16[1152,768]{1,0:T(8,128)(2,1)}, bf16[1152,768]{1,0:T(8,128)(2,1)}, bf16[768,1152]{1,0:T(8,128)(2,1)}, bf16[144,768]{1,0:T(8,128)(2,1)}, bf16...) custom-call(bf16[4096,1152]{1,0:T(8,128)(2,1)} %bitcast.63, ...), custom_call_target="tpu_custom_call" | custom-call | flops 28991029248 | tf_op jit(solution)/shard_map/by_hidden/pallas_call | solution.py:233
  622.9 47.7 %last.1 = (bf16[144,768]{1,0:T(8,128)(2,1)}, bf16[144,768]{1,0:T(8,128)(2,1)}, bf16[144,768]{1,0:T(8,128)(2,1)}, bf16[144,768]{1,0:T(8,128)(2,1)}, bf16[2,96,1152]{2,1,0:T(8,128)(2,1)}) custom-call(bf16[8,144,768]{2,1,0:T(8,128)(2,1)} %bitcast.46, bf16[8,144,768]{2,1,0:T(8,128)(2,1)} %bitcast.47, bf16[8,96,1152]{2,1,0:T(8,128)(2,1)} %bitcast.48), custom_call_target="tpu_custom_call" | custom-call | tf_op jit(solution)/shard_map/last/pallas_call | solution.py:233
  670.6 28.5 %adamw.1 = (bf16[2,144,4608]{2,1,0:T(8,128)(2,1)}, bf16[2,144,4608]{2,1,0:T(8,128)(2,1)}, bf16[2,576,1152]{2,1,0:T(8,128)(2,1)}, f32[2,144,4608]{2,1,0:T(8,128)}...) custom-call(bf16[2,144,4608]{2,1,0:T(8,128)(2,1)} %refs_0_.1, ...), custom_call_target="tpu_custom_call" | custom-call | tf_op jit(solution)/shard_map/adamw/pallas_call | solution.py:578

commit v3 on v2

--- a/solution.py
+++ b/solution.py
@@ -187,10 +187,19 @@
             self.tell.wait()
 
 
-def run(name, cid, compute, grid, ins, in_specs, outs, out_specs, scratch=(), comms=(), bits=(), when=(0.4, 0.5), flops=0, start=0):
+def run(name, cid, compute, grid, ins, in_specs, outs, out_specs, scratch=(), comms=(), bits=(), when=(0.4, 0.5), flops=0, start=0, resident=(), closing=None):
     steps = math.prod(grid)
     bits = sorted(set(bits).union(*(comm.bits for comm in comms)))
     middle, late = (min(steps - 1, int(steps * w)) for w in when)
+    if not bits:
+        for a, i in resident:
+            shape = a.shape if i is None else (a.shape[0], None, *a.shape[2:])
+            place = (0,) * a.ndim if i is None else (0, i) + (0,) * (a.ndim - 2)
+            ins, in_specs = [*ins, a], [*in_specs, pl.BlockSpec(shape, lambda *_, place=place: place, pipeline_mode=pl.Buffered(1))]
+        resident = ()
+    ins, in_specs, scratch = list(ins) + [a for a, _ in resident], list(in_specs) + [ANY] * len(resident), list(scratch)
+    parts_of = [jax.eval_shape(lambda a, i=i: a if i is None else a[:, i], a) for a, i in resident]
+    scratch += [pltpu.VMEM(a.shape, a.dtype) for a in parts_of] + [pltpu.SemaphoreType.DMA((len(resident),))] * bool(resident)
     counts = [len(ins)] + [len(c.ins) for c in comms] + [len(outs)] + [len(c.outs) for c in comms] + [len(scratch)] + [len(c.scratch) for c in comms]
 
     def kernel(*refs):
@@ -202,17 +211,35 @@
         for axis, size in enumerate(grid):
             step = step * size + pl.program_id(axis)
         k = len(comms) + 1
+        held = len(resident)
         own = groups[0], groups[k], groups[2 * k]
-        for n, comm in enumerate(comms):
-            comm.bind(groups[1 + n], groups[k + 1 + n], groups[2 * k + 1 + n], own)
+        if held:
+            here, own_scratch, sems = own[2][-held - 1 : -1], own[2][: -held - 1], own[2][-1]
+            sources = own[0][-held:]
+            own = own[0][:-held] + here, own[1], own_scratch
+
+        def bring():
+            for n, (_, i) in enumerate(resident):
+                yield pltpu.make_async_copy(sources[n] if i is None else sources[n].at[:, i], here[n], sems.at[n])
 
         def do(*names):
+            for n, comm in enumerate(comms):
+                comm.bind(groups[1 + n], groups[k + 1 + n], groups[2 * k + 1 + n], own)
             for what in names:
+                if what == "end":
+                    for comm, before in zip([*comms, None], [None, *comms], strict=True):
+                        if comm:
+                            comm.end()
+                        if before:
+                            before.finish()
+                    continue
                 for comm in comms:
                     getattr(comm, what)()
 
         @pl.when(step == 0)
         def _():
+            for copy in bring():
+                copy.start()
             if bits:
                 barrier = pltpu.get_barrier_semaphore()
                 for bit in bits:
@@ -220,14 +247,22 @@
                 pl.semaphore_wait(barrier, len(bits))
             if not start:
                 do("begin", "more")
+            for copy in bring():
+                copy.wait()
 
         compute(*own)
-        for at, what in ((start, ("begin", "more")), (middle, ("middle",)), (late, ("late",)), (steps - 1, ("end", "finish", "close"))):
+        for at, what in ((start, ("begin", "more")), (middle, ("middle",)), (late, ("late",)), (steps - 1, ("end", "close"))):
             if comms and (start or at or what[0] != "begin"):
 
                 @pl.when(step == at)
                 def _():
                     do(*what)
+
+        if closing:
+
+            @pl.when(step == steps - 1)
+            def _():
+                closing(*own)
 
     params = dict(collective_id=cid, has_side_effects=True) if bits else {}
     results = pl.pallas_call(
@@ -277,23 +312,23 @@
 
         def up_of(a, w, gate, fetch):
             def compute(ins, outs, _):
-                up, gate = mm(ins[0][...], ins[1][...]), ins[2][...]
+                up, gate = mm(ins[0][...], ins[2][...]), ins[1][...]
                 outs[0][...] = up
                 outs[1][...] = (jax.nn.silu(gate) * up).astype(BF16)
 
             tile = lambda n: pl.BlockSpec((TILE, n), lambda t: (t, 0))
-            whole = pl.BlockSpec((d, half), lambda t: (0, 0), pipeline_mode=pl.Buffered(1))
             (up, hidden), ((got,),) = run(
                 "up",
                 next(cid),
                 compute,
                 (every // TILE,),
-                [a, w, gate],
-                [tile(d), whole, tile(half)],
+                [a, gate],
+                [tile(d), tile(half)],
                 [f32_rows, bf16_rows],
                 [tile(half)] * 2,
                 comms=[fetch],
                 flops=unit,
+                resident=[(w, None)],
             )
             return up, hidden, got
 
@@ -304,7 +339,7 @@
             def compute(ins, outs, scratch):
                 sent, came, state, ssem, rsem, ssem2, rsem2, local = scratch
                 t = pl.program_id(0)
-                product = lambda: terms(ins[: len(lhs)], ins[len(lhs) : len(lhs) + len(rhs)])
+                product = lambda: terms(ins[: len(lhs)], ins[len(lhs) + len(given) :])
                 away = lambda n: remote(sent.at[n], came.at[n], (ssem, rsem), n, 1)
                 shared = outs[-1]
                 rows_of = lambda n: pl.ds(pl.multiple_of(n * TILE, TILE), TILE)
@@ -328,7 +363,7 @@
                 @pl.when(n >= 0)
                 def _():
                     away(n).wait_recv()
-                    results = finish(product() + came[n], *[g[...] for g in ins[len(lhs) + len(rhs) :]])
+                    results = finish(product() + came[n], *[g[...] for g in ins[len(lhs) : len(lhs) + len(given)]])
                     for out, result in zip(outs[:-1], results[:-1], strict=True):
                         out[...] = result
                     state[n] = results[-1]
@@ -343,20 +378,20 @@
                         save(n).wait()
 
             scratch = [pltpu.VMEM((tiles, TILE, d), F32)] * 2 + [pltpu.VMEM((tiles, TILE, d), BF16)] + [pltpu.SemaphoreType.DMA((tiles,))] * 5
-            whole = lambda a: pl.BlockSpec(a.shape, lambda t: (0,) * a.ndim, pipeline_mode=pl.Buffered(1))
             results, got = run(
                 name,
                 next(cid),
                 compute,
                 (2 * tiles,),
-                [*lhs, *rhs, *given],
-                list(lhs_specs) + [whole(a) for a in rhs] + [here] * len(given),
+                [*lhs, *given],
+                list(lhs_specs) + [here] * len(given),
                 [jax.ShapeDtypeStruct((tokens, d), BF16)] * keep + [jax.ShapeDtypeStruct((2, tokens, d), BF16)],
                 [here] * keep + [ANY],
                 scratch,
                 comms=comms,
                 bits=(1,),
-                flops=unit * len(lhs),
+                flops=unit,
+                resident=[(a, None) for a in rhs],
             )
             return [*results[:-1], results[-1].reshape(every, d)], got
 
@@ -373,15 +408,22 @@
             (h, a), got = over_cores("down", terms, [hidden], [swapped(half)], [w.reshape(chips, PARTS, share, d)], [h], finish, 1, fetches)
             return h, a, got
 
-        def by_hidden(by_h, a, given, given_specs, start, keep, comms=()):
+        def by_hidden(by_h, a, given, given_specs, resident, start, keep, comms=()):
             n_steps = every // TILE
+
+            def written(outs, scratch):
+                return [pltpu.make_async_copy(scratch[3 + i], outs[i], scratch[6].at[i]) for i in range(3)]
+
+            def closing(ins, outs, scratch):
+                for copy in written(outs, scratch):
+                    copy.wait()
 
             def compute(ins, outs, scratch):
                 t = pl.program_id(0)
 
                 @pl.when(t == 0)
                 def _():
-                    for acc in scratch:
+                    for acc in scratch[:3]:
                         acc[...] = jnp.zeros_like(acc)
 
                 by_h, a = ins[0][...], ins[1][...]
@@ -393,17 +435,19 @@
                 hidden = (act * up).astype(BF16)
                 if keep:
                     outs[3][...], outs[4][...] = by_gate, by_up
-                for acc, lhs, rhs in zip(scratch, (a, a, hidden), (by_gate, by_up, by_h), strict=True):
+                for acc, lhs, rhs in zip(scratch[:3], (a, a, hidden), (by_gate, by_up, by_h), strict=True):
                     acc[...] += t_mm(lhs, rhs)
 
                 @pl.when(t == n_steps - 1)
                 def _():
-                    for acc, out in zip(scratch, outs[:3], strict=True):
-                        out[...] = acc[...].astype(BF16)
+                    for i in range(3):
+                        scratch[3 + i][...] = scratch[i][...].astype(BF16)
+                    for copy in written(outs, scratch):
+                        copy.start()
 
             tile = lambda n: pl.BlockSpec((TILE, n), lambda t: (t, 0))
             outs = [jax.ShapeDtypeStruct((d, part), BF16)] * 2 + [jax.ShapeDtypeStruct((part, d), BF16)]
-            out_specs = [whole(d, part)] * 2 + [whole(part, d)]
+            out_specs = [ANY] * 3
             if keep:
                 outs += [jax.ShapeDtypeStruct((every, part), BF16)] * 2
                 out_specs += [tile(part)] * 2
@@ -416,26 +460,25 @@
                 [tile(d), tile(d), *given_specs],
                 outs,
                 out_specs,
-                [pltpu.VMEM((d, part), F32)] * 2 + [pltpu.VMEM((part, d), F32)],
+                [pltpu.VMEM(s, t) for t in (F32, BF16) for s in ((d, part), (d, part), (part, d))] + [pltpu.SemaphoreType.DMA((3,))],
+                closing=closing,
                 comms=comms,
                 flops=(6 if keep else 4) * unit // PARTS,
+                resident=resident,
             )
-
-        whole = lambda *s: pl.BlockSpec(s, lambda t: (0,) * len(s), pipeline_mode=pl.Buffered(1))
 
         def by_last(by_h, a, wg, wu, wd, comms):
             def start(by_h, a, wg, wu, wd):
                 return mm(a, wg), mm(a, wu), mm_t(by_h, wd).astype(BF16).astype(F32)
 
-            return by_hidden(by_h, a, [wg, wu, wd], [whole(d, part)] * 2 + [whole(part, d)], start, True, comms)
+            return by_hidden(by_h, a, [], [], [(wg, None), (wu, None), (wd, None)], start, True, comms)
 
         def by_first(p, by_h, a, gate, up, wd, comms):
             def start(by_h, a, gate, up, wd):
                 return gate, up, mm_t(by_h, wd.reshape(part, d)).astype(BF16).astype(F32)
 
             piece = pl.BlockSpec((TILE, part), lambda t: (t, p))
-            rows_of = pl.BlockSpec((chips, 1, share, d), lambda t: (0, p, 0, 0), pipeline_mode=pl.Buffered(1))
-            return by_hidden(by_h, a, [gate, up, wd.reshape(chips, PARTS, share, d)], [piece, piece, rows_of], start, False, comms)
+            return by_hidden(by_h, a, [gate, up], [piece, piece], [(wd.reshape(chips, PARTS, share, d), p)], start, False, comms)
 
         def by_input(by_gates, by_ups, wg, wu, h, by_h, comms=()):
             def terms(lhs, rhs):
@@ -488,7 +531,7 @@
                             keep(m).start()
                             pass_on(m).start()
 
-                @pl.when(s == 2)
+                @pl.when(s == 1)
                 def _():
                     keep(0).wait()
                     pass_on(0).wait_recv()
@@ -536,7 +579,7 @@
                 comms=[Gather(jax.ShapeDtypeStruct((2, rows, half), BF16), lambda own: own[1][0])],
                 bits=(1,),
                 when=(0.999, 0.999),
-                start=2,
+                start=1,
             )
             return blocks, a.reshape(every, d), dys.reshape(every, d), got
 

time: 706 us -> 686 us (0.972)
  Pallas kernels: 698 us -> 678 us
    pallas_call x12, Pallas kernels: 670 us -> 650 us  [run(): pl.pallas_call(kernel, name=name, grid=grid, in_specs=list(in_specs) + [A...]
where the time goes in v3:
time: 686 us; the launch traced here: 679 us
  Pallas kernels  678 us (99%)
    pallas_call x12, Pallas kernels, run(): pl.pallas_call(kernel, name=name, grid=grid, in_specs=list(in_specs) + [A...  650 us
    pallas_call x1, Pallas kernels, updated(): pl.pallas_call(kernel, name='adamw', grid=(layers, PARTS), in_specs=[bloc...  28.5 us

profile of v3, /device:TPU:0, one launch (start us, length us, event | category | flops | bytes accessed | tf_op | source)
XLA Modules:
  0.0 679.5 jit_solution(17834093279559701925)
XLA Ops:
  0.6 53.6 %open.1 = (bf16[2,144,2304]{2,1,0:T(8,128)(2,1)}, bf16[2,144,2304]{2,1,0:T(8,128)(2,1)}, bf16[2,144,768]{2,1,0:T(8,128)(2,1)}, bf16[2,144,768]{2,1,0:T(8,128)(2,...) custom-call(bf16[2048,1152]{1,0:T(8,128)(2,1)} %bitcast.38, ...), custom_call_target="tpu_custom_call" | custom-call | tf_op jit(solution)/shard_map/open/pallas_call | solution.py:268
  54.2 49.5 %gate.1 = (f32[4096,2304]{1,0:T(8,128)}, bf16[8,144,2304]{2,1,0:T(8,128)(2,1)}) custom-call(bf16[4096,1152]{1,0:T(8,128)(2,1)} %bitcast.49, bf16[1152,2304]{1,0:T(8,128)(2,1)} %bitcast.57, bf16[2,144,2304]{2,1,0:T(8,128)(2,1)} %get-tuple-element.93.refs_2_), custom_call_target="tpu_custom_call" | custom-call | flops 21743271936 | tf_op jit(solution)/shard_map/gate/pallas_call | solution.py:268
  103.8 50.4 %up.1 = (f32[4096,2304]{1,0:T(8,128)}, bf16[4096,2304]{1,0:T(8,128)(2,1)}, bf16[8,288,1152]{2,1,0:T(8,128)(2,1)}) custom-call(bf16[4096,1152]{1,0:T(8,128)(2,1)} %bitcast.50, f32[4096,2304]{1,0:T(8,128)} %get-tuple-element.94.refs_1_.refs_2_, bf16[1152,2304]{1,0:T(8,128)(2,1)} %bitcast.68, bf16[2,2,288,1152]{3,2,1,0:T(8,128)(2,1)} %bitcast.42), custom_call_target="tpu_custom_call" | custom-call | flops 21743271936 | tf_op jit(solution)/shard_map/up/pallas_call | solution.py:268
  154.2 48.6 %down.1 = (bf16[2048,1152]{1,0:T(8,128)(2,1)}, bf16[2,2048,1152]{2,1,0:T(8,128)(2,1)}, bf16[8,144,768]{2,1,0:T(8,128)(2,1)}, bf16[8,144,768]{2,1,0:T(8,128)(2,1)}, bf16[8,96,1152]{2,1,0:T(8,128)(2,1)}) custom-call(bf16[4096,2304]{1,0:T(8,128)(2,1)} %get-tuple-element.96.refs_0_, bf16[2048,1152]{1,0:T(8,128)(2,1)} %bitcast.39, ...), custom_call_target="tpu_custom_call" | custom-call | flops 21743271936 | tf_op jit(solution)/shard_map/down/pallas_call | solution.py:268
  202.8 61.9 %by_hidden.6 = (bf16[1152,768]{1,0:T(8,128)(2,1)}, bf16[1152,768]{1,0:T(8,128)(2,1)}, bf16[768,1152]{1,0:T(8,128)(2,1)}, bf16[4096,768]{1,0:T(8,128)(2,1)}, bf16...) custom-call(bf16[4096,1152]{1,0:T(8,128)(2,1)} %bitcast.54, ...), custom_call_target="tpu_custom_call" | custom-call | flops 43486543872 | tf_op jit(solution)/shard_map/by_hidden/pallas_call | solution.py:268
  264.7 65.2 %by_hidden.7 = (bf16[1152,768]{1,0:T(8,128)(2,1)}, bf16[1152,768]{1,0:T(8,128)(2,1)}, bf16[768,1152]{1,0:T(8,128)(2,1)}, bf16[4096,768]{1,0:T(8,128)(2,1)}, bf16...) custom-call(bf16[4096,1152]{1,0:T(8,128)(2,1)} %bitcast.55, ...), custom_call_target="tpu_custom_call" | custom-call | flops 43486543872 | tf_op jit(solution)/shard_map/by_hidden/pallas_call | solution.py:268
  330.0 65.1 %by_hidden.8 = (bf16[1152,768]{1,0:T(8,128)(2,1)}, bf16[1152,768]{1,0:T(8,128)(2,1)}, bf16[768,1152]{1,0:T(8,128)(2,1)}, bf16[4096,768]{1,0:T(8,128)(2,1)}, bf16...) custom-call(bf16[4096,1152]{1,0:T(8,128)(2,1)} %bitcast.56, ...), custom_call_target="tpu_custom_call" | custom-call | flops 43486543872 | tf_op jit(solution)/shard_map/by_hidden/pallas_call | solution.py:268
  395.1 66.6 %by_input.1 = (bf16[2,2048,1152]{2,1,0:T(8,128)(2,1)}, bf16[144,768]{1,0:T(8,128)(2,1)}, bf16[144,768]{1,0:T(8,128)(2,1)}, bf16[144,768]{1,0:T(8,128)(2,1)}, bf1...) custom-call(bf16[4096,768]{1,0:T(8,128)(2,1)} %get-tuple-element.107.refs_0_, ...), custom_call_target="tpu_custom_call" | custom-call | flops 21743271936 | tf_op jit(solution)/shard_map/by_input/pallas_call | solution.py:268
  461.7 41.1 %by_hidden.9 = (bf16[1152,768]{1,0:T(8,128)(2,1)}, bf16[1152,768]{1,0:T(8,128)(2,1)}, bf16[768,1152]{1,0:T(8,128)(2,1)}) custom-call(bf16[4096,1152]{1,0:T(8,128)(2,1)} %bitcast.61, bf16[4096,1152]{1,0:T(8,128)(2,1)} %bitcast.51, f32[4096,2304]{1,0:T(8,128)} %get-tuple-element.94.refs_1_.refs_2_, f32[4096,2304]{1,0:T(8,128)} %get-tuple-element.131.refs_3_, ...), custom_call_target="tpu_custom_call" | custom-call | flops 28991029248 | tf_op jit(solution)/shard_map/by_hidden/pallas_call | solution.py:268
  502.8 50.0 %by_hidden.10 = (bf16[1152,768]{1,0:T(8,128)(2,1)}, bf16[1152,768]{1,0:T(8,128)(2,1)}, bf16[768,1152]{1,0:T(8,128)(2,1)}, bf16[144,768]{1,0:T(8,128)(2,1)}, bf16...) custom-call(bf16[4096,1152]{1,0:T(8,128)(2,1)} %bitcast.62, ...), custom_call_target="tpu_custom_call" | custom-call | flops 28991029248 | tf_op jit(solution)/shard_map/by_hidden/pallas_call | solution.py:268
  552.8 50.3 %by_hidden.11 = (bf16[1152,768]{1,0:T(8,128)(2,1)}, bf16[1152,768]{1,0:T(8,128)(2,1)}, bf16[768,1152]{1,0:T(8,128)(2,1)}, bf16[144,768]{1,0:T(8,128)(2,1)}, bf16...) custom-call(bf16[4096,1152]{1,0:T(8,128)(2,1)} %bitcast.63, ...), custom_call_target="tpu_custom_call" | custom-call | flops 28991029248 | tf_op jit(solution)/shard_map/by_hidden/pallas_call | solution.py:268
  603.1 47.4 %last.1 = (bf16[144,768]{1,0:T(8,128)(2,1)}, bf16[144,768]{1,0:T(8,128)(2,1)}, bf16[144,768]{1,0:T(8,128)(2,1)}, bf16[144,768]{1,0:T(8,128)(2,1)}, bf16[2,96,1152]{2,1,0:T(8,128)(2,1)}) custom-call(bf16[8,144,768]{2,1,0:T(8,128)(2,1)} %bitcast.46, bf16[8,144,768]{2,1,0:T(8,128)(2,1)} %bitcast.47, bf16[8,96,1152]{2,1,0:T(8,128)(2,1)} %bitcast.48), custom_call_target="tpu_custom_call" | custom-call | tf_op jit(solution)/shard_map/last/pallas_call | solution.py:268
  650.5 28.5 %adamw.1 = (bf16[2,144,4608]{2,1,0:T(8,128)(2,1)}, bf16[2,144,4608]{2,1,0:T(8,128)(2,1)}, bf16[2,576,1152]{2,1,0:T(8,128)(2,1)}, f32[2,144,4608]{2,1,0:T(8,128)}...) custom-call(bf16[2,144,4608]{2,1,0:T(8,128)(2,1)} %refs_0_.1, ...), custom_call_target="tpu_custom_call" | custom-call | tf_op jit(solution)/shard_map/adamw/pallas_call | solution.py:621

commit v4 on v3

--- a/solution.py
+++ b/solution.py
@@ -13,6 +13,8 @@
 ANY = pl.BlockSpec(memory_space=pl.ANY)
 PARTS = 3
 TILE = 512
+CORE, Y, X = 1, 2, 4
+HERE, LOW, HIGH = 0, 0, 1
 
 
 def mm(a, w):
@@ -62,7 +64,7 @@
 
 
 class Gather:
-    bits = (2, 4)
+    bits = (Y, X)
 
     def __init__(self, block, source=None, index=None):
         _, r, n = block.shape[-3:]
@@ -77,14 +79,9 @@
         block = self.source(own) if self.source else ins[0] if self.index is None else ins[0].at[self.index]
         chip = lax.axis_index("dp") // 2
         at = lambda bit, half: full.at[other(chip, bit) * 2 + half] if bit else full.at[chip * 2 + half]
-        self.copies = [
-            remote(block.at[1], at(0, 1), sems, 0, 2),
-            remote(block.at[0], at(0, 0), sems, 1, 4),
-            remote(block.at[0], at(0, 0), sems, 2, 2),
-            remote(block.at[1], at(0, 1), sems, 3, 4),
-            remote(at(2, 0), at(2, 0), sems, 4, 2),
-            remote(at(1, 1), at(1, 1), sems, 5, 4),
-        ]
+        moves = [(block.at[half], at(HERE, half), bit) for half, bit in ((HIGH, Y), (LOW, X), (LOW, Y), (HIGH, X))]
+        moves += [(at(*near), at(*near), bit) for near, bit in (((X // 2, LOW), Y), ((Y // 2, HIGH), X))]
+        self.copies = [remote(source, to, sems, n, bit) for n, (source, to, bit) in enumerate(moves)]
         self.own = [pltpu.make_async_copy(block, held, local.at[0]), pltpu.make_async_copy(held, full.at[pl.ds(chip * 2, 2)], local.at[1])]
 
     def begin(self):
@@ -107,8 +104,8 @@
         pass
 
     def end(self):
-        for n in (2, 3, 4, 5):
-            self.copies[n].wait_recv()
+        for copy in self.copies[2:]:
+            copy.wait_recv()
 
     def finish(self):
         pass
@@ -120,7 +117,7 @@
 
 
 class Scatter:
-    bits = (1, 2, 4)
+    bits = (CORE, Y, X)
 
     def __init__(self, blocks, rows):
         _, r, n = blocks.shape
@@ -134,15 +131,11 @@
         at = lambda bit, half: blocks.at[other(chip, bit) * 2 + half]
         diagonal = lambda half: blocks.at[(3 - chip) * 2 + half]
         self.came, self.mine, self.total, self.by_y, self.by_x, self.held = came, mine, total, by_y, by_x, held
-        self.copies = [
-            remote(diagonal(0), came.at[0], sems, 0, 4),
-            remote(diagonal(1), came.at[1], sems, 1, 2),
-            remote(at(2, 0), by_x.at[0], sems, 2, 4),
-            remote(at(1, 1), by_y.at[1], sems, 3, 2),
-            remote(total.at[0], by_y.at[0], sems, 4, 2),
-            remote(total.at[1], by_x.at[1], sems, 5, 4),
-        ]
-        self.own = [pltpu.make_async_copy(at(1, 0), mine.at[0], local.at[0]), pltpu.make_async_copy(at(2, 1), mine.at[1], local.at[1])]
+        moves = [(diagonal(half), came.at[half], bit) for half, bit in ((LOW, X), (HIGH, Y))]
+        moves += [(at(bit // 2, half), to.at[half], bit) for half, bit, to in ((LOW, X, by_x), (HIGH, Y, by_y))]
+        moves += [(total.at[half], to.at[half], bit) for half, bit, to in ((LOW, Y, by_y), (HIGH, X, by_x))]
+        self.copies = [remote(source, to, sems, n, bit) for n, (source, to, bit) in enumerate(moves)]
+        self.own = [pltpu.make_async_copy(at(bit // 2, half), mine.at[half], local.at[half]) for half, bit in ((LOW, Y), (HIGH, X))]
         self.own += [pltpu.make_async_copy(blocks.at[pl.ds(chip * 2, 2)], held, local.at[2])]
         if self.rows:
             self.out = pltpu.make_async_copy(held.at[core], outs[0], local.at[3])
@@ -169,8 +162,8 @@
         self.copies[5].start()
 
     def end(self):
-        for n in (2, 3, 4, 5):
-            self.copies[n].wait_recv()
+        for copy in self.copies[2:]:
+            copy.wait_recv()
         self.own[2].wait()
         self.held[...] = (self.held[...].astype(F32) + self.by_y[...].astype(F32) + self.by_x[...].astype(F32)).astype(BF16)
 
@@ -336,15 +329,24 @@
             tiles = tokens // TILE
             here = pl.BlockSpec((TILE, d), lambda t: (jnp.maximum(t - tiles, 0), 0))
 
+            def moves(outs, scratch):
+                sent, came, state, ssem, rsem, ssem2, rsem2, local = scratch
+                rows_of = lambda n: pl.ds(pl.multiple_of(n * TILE, TILE), TILE)
+                away = lambda n: remote(sent.at[n], came.at[n], (ssem, rsem), n, CORE)
+                tell = lambda n: remote(state.at[n], outs[-1].at[1, rows_of(n)], (ssem2, rsem2), n, CORE)
+                save = lambda n: pltpu.make_async_copy(state.at[n], outs[-1].at[0, rows_of(n)], local.at[n])
+                return away, tell, save
+
+            def closing(ins, outs, scratch):
+                for n in range(tiles):
+                    for copy, wait in zip(moves(outs, scratch), ("wait_send", "wait", "wait"), strict=True):
+                        getattr(copy(n), wait)()
+
             def compute(ins, outs, scratch):
-                sent, came, state, ssem, rsem, ssem2, rsem2, local = scratch
+                sent, came, state = scratch[:3]
                 t = pl.program_id(0)
                 product = lambda: terms(ins[: len(lhs)], ins[len(lhs) + len(given) :])
-                away = lambda n: remote(sent.at[n], came.at[n], (ssem, rsem), n, 1)
-                shared = outs[-1]
-                rows_of = lambda n: pl.ds(pl.multiple_of(n * TILE, TILE), TILE)
-                tell = lambda n: remote(state.at[n], shared.at[1, rows_of(n)], (ssem2, rsem2), n, 1)
-                save = lambda n: pltpu.make_async_copy(state.at[n], shared.at[0, rows_of(n)], local.at[n])
+                away, tell, save = moves(outs, scratch)
                 n = t - tiles
 
                 @pl.when((t > 0) & (t <= tiles))
@@ -372,10 +374,6 @@
                 def _():
                     tell(tiles - 1).start()
                     save(tiles - 1).start()
-                    for n in range(tiles):
-                        away(n).wait_send()
-                        tell(n).wait()
-                        save(n).wait()
 
             scratch = [pltpu.VMEM((tiles, TILE, d), F32)] * 2 + [pltpu.VMEM((tiles, TILE, d), BF16)] + [pltpu.SemaphoreType.DMA((tiles,))] * 5
             results, got = run(
@@ -392,6 +390,7 @@
                 bits=(1,),
                 flops=unit,
                 resident=[(a, None) for a in rhs],
+                closing=closing,
             )
             return [*results[:-1], results[-1].reshape(every, d)], got
 

time: 686 us -> 685 us (level)
  no operation moved by 1% of the time
where the time goes in v4:
time: 685 us; the launch traced here: 678 us
  Pallas kernels  677 us (99%)
    pallas_call x12, Pallas kernels, run(): pl.pallas_call(kernel, name=name, grid=grid, in_specs=list(in_specs) + [A...  648 us
    pallas_call x1, Pallas kernels, updated(): pl.pallas_call(kernel, name='adamw', grid=(layers, PARTS), in_specs=[bloc...  28.5 us

profile of v4, /device:TPU:0, one launch (start us, length us, event | category | flops | bytes accessed | tf_op | source)
XLA Modules:
  0.0 678.2 jit_solution(11202170524094172134)
XLA Ops:
  0.6 53.6 %open.1 = (bf16[2,144,2304]{2,1,0:T(8,128)(2,1)}, bf16[2,144,2304]{2,1,0:T(8,128)(2,1)}, bf16[2,144,768]{2,1,0:T(8,128)(2,1)}, bf16[2,144,768]{2,1,0:T(8,128)(2,...) custom-call(bf16[2048,1152]{1,0:T(8,128)(2,1)} %bitcast.38, ...), custom_call_target="tpu_custom_call" | custom-call | tf_op jit(solution)/shard_map/open/pallas_call | solution.py:261
  54.2 49.5 %gate.1 = (f32[4096,2304]{1,0:T(8,128)}, bf16[8,144,2304]{2,1,0:T(8,128)(2,1)}) custom-call(bf16[4096,1152]{1,0:T(8,128)(2,1)} %bitcast.49, bf16[1152,2304]{1,0:T(8,128)(2,1)} %bitcast.57, bf16[2,144,2304]{2,1,0:T(8,128)(2,1)} %get-tuple-element.93.refs_2_), custom_call_target="tpu_custom_call" | custom-call | flops 21743271936 | tf_op jit(solution)/shard_map/gate/pallas_call | solution.py:261
  103.8 50.4 %up.1 = (f32[4096,2304]{1,0:T(8,128)}, bf16[4096,2304]{1,0:T(8,128)(2,1)}, bf16[8,288,1152]{2,1,0:T(8,128)(2,1)}) custom-call(bf16[4096,1152]{1,0:T(8,128)(2,1)} %bitcast.50, f32[4096,2304]{1,0:T(8,128)} %get-tuple-element.94.refs_1_.refs_2_, bf16[1152,2304]{1,0:T(8,128)(2,1)} %bitcast.68, bf16[2,2,288,1152]{3,2,1,0:T(8,128)(2,1)} %bitcast.42), custom_call_target="tpu_custom_call" | custom-call | flops 21743271936 | tf_op jit(solution)/shard_map/up/pallas_call | solution.py:261
  154.2 48.6 %down.1 = (bf16[2048,1152]{1,0:T(8,128)(2,1)}, bf16[2,2048,1152]{2,1,0:T(8,128)(2,1)}, bf16[8,144,768]{2,1,0:T(8,128)(2,1)}, bf16[8,144,768]{2,1,0:T(8,128)(2,1)}, bf16[8,96,1152]{2,1,0:T(8,128)(2,1)}) custom-call(bf16[4096,2304]{1,0:T(8,128)(2,1)} %get-tuple-element.96.refs_0_, bf16[2048,1152]{1,0:T(8,128)(2,1)} %bitcast.39, ...), custom_call_target="tpu_custom_call" | custom-call | flops 21743271936 | tf_op jit(solution)/shard_map/down/pallas_call | solution.py:261
  202.8 61.9 %by_hidden.6 = (bf16[1152,768]{1,0:T(8,128)(2,1)}, bf16[1152,768]{1,0:T(8,128)(2,1)}, bf16[768,1152]{1,0:T(8,128)(2,1)}, bf16[4096,768]{1,0:T(8,128)(2,1)}, bf16...) custom-call(bf16[4096,1152]{1,0:T(8,128)(2,1)} %bitcast.54, ...), custom_call_target="tpu_custom_call" | custom-call | flops 43486543872 | tf_op jit(solution)/shard_map/by_hidden/pallas_call | solution.py:261
  264.8 65.2 %by_hidden.7 = (bf16[1152,768]{1,0:T(8,128)(2,1)}, bf16[1152,768]{1,0:T(8,128)(2,1)}, bf16[768,1152]{1,0:T(8,128)(2,1)}, bf16[4096,768]{1,0:T(8,128)(2,1)}, bf16...) custom-call(bf16[4096,1152]{1,0:T(8,128)(2,1)} %bitcast.55, ...), custom_call_target="tpu_custom_call" | custom-call | flops 43486543872 | tf_op jit(solution)/shard_map/by_hidden/pallas_call | solution.py:261
  330.0 65.1 %by_hidden.8 = (bf16[1152,768]{1,0:T(8,128)(2,1)}, bf16[1152,768]{1,0:T(8,128)(2,1)}, bf16[768,1152]{1,0:T(8,128)(2,1)}, bf16[4096,768]{1,0:T(8,128)(2,1)}, bf16...) custom-call(bf16[4096,1152]{1,0:T(8,128)(2,1)} %bitcast.56, ...), custom_call_target="tpu_custom_call" | custom-call | flops 43486543872 | tf_op jit(solution)/shard_map/by_hidden/pallas_call | solution.py:261
  395.1 65.4 %by_input.1 = (bf16[2,2048,1152]{2,1,0:T(8,128)(2,1)}, bf16[144,768]{1,0:T(8,128)(2,1)}, bf16[144,768]{1,0:T(8,128)(2,1)}, bf16[144,768]{1,0:T(8,128)(2,1)}, bf1...) custom-call(bf16[4096,768]{1,0:T(8,128)(2,1)} %get-tuple-element.107.refs_0_, ...), custom_call_target="tpu_custom_call" | custom-call | flops 21743271936 | tf_op jit(solution)/shard_map/by_input/pallas_call | solution.py:261
  460.5 41.1 %by_hidden.9 = (bf16[1152,768]{1,0:T(8,128)(2,1)}, bf16[1152,768]{1,0:T(8,128)(2,1)}, bf16[768,1152]{1,0:T(8,128)(2,1)}) custom-call(bf16[4096,1152]{1,0:T(8,128)(2,1)} %bitcast.61, bf16[4096,1152]{1,0:T(8,128)(2,1)} %bitcast.51, f32[4096,2304]{1,0:T(8,128)} %get-tuple-element.94.refs_1_.refs_2_, f32[4096,2304]{1,0:T(8,128)} %get-tuple-element.131.refs_3_, ...), custom_call_target="tpu_custom_call" | custom-call | flops 28991029248 | tf_op jit(solution)/shard_map/by_hidden/pallas_call | solution.py:261
  501.6 49.9 %by_hidden.10 = (bf16[1152,768]{1,0:T(8,128)(2,1)}, bf16[1152,768]{1,0:T(8,128)(2,1)}, bf16[768,1152]{1,0:T(8,128)(2,1)}, bf16[144,768]{1,0:T(8,128)(2,1)}, bf16...) custom-call(bf16[4096,1152]{1,0:T(8,128)(2,1)} %bitcast.62, ...), custom_call_target="tpu_custom_call" | custom-call | flops 28991029248 | tf_op jit(solution)/shard_map/by_hidden/pallas_call | solution.py:261
  551.5 50.3 %by_hidden.11 = (bf16[1152,768]{1,0:T(8,128)(2,1)}, bf16[1152,768]{1,0:T(8,128)(2,1)}, bf16[768,1152]{1,0:T(8,128)(2,1)}, bf16[144,768]{1,0:T(8,128)(2,1)}, bf16...) custom-call(bf16[4096,1152]{1,0:T(8,128)(2,1)} %bitcast.63, ...), custom_call_target="tpu_custom_call" | custom-call | flops 28991029248 | tf_op jit(solution)/shard_map/by_hidden/pallas_call | solution.py:261
  601.8 47.4 %last.1 = (bf16[144,768]{1,0:T(8,128)(2,1)}, bf16[144,768]{1,0:T(8,128)(2,1)}, bf16[144,768]{1,0:T(8,128)(2,1)}, bf16[144,768]{1,0:T(8,128)(2,1)}, bf16[2,96,1152]{2,1,0:T(8,128)(2,1)}) custom-call(bf16[8,144,768]{2,1,0:T(8,128)(2,1)} %bitcast.46, bf16[8,144,768]{2,1,0:T(8,128)(2,1)} %bitcast.47, bf16[8,96,1152]{2,1,0:T(8,128)(2,1)} %bitcast.48), custom_call_target="tpu_custom_call" | custom-call | tf_op jit(solution)/shard_map/last/pallas_call | solution.py:261
  649.2 28.5 %adamw.1 = (bf16[2,144,4608]{2,1,0:T(8,128)(2,1)}, bf16[2,144,4608]{2,1,0:T(8,128)(2,1)}, bf16[2,576,1152]{2,1,0:T(8,128)(2,1)}, f32[2,144,4608]{2,1,0:T(8,128)}...) custom-call(bf16[2,144,4608]{2,1,0:T(8,128)(2,1)} %refs_0_.1, ...), custom_call_target="tpu_custom_call" | custom-call | tf_op jit(solution)/shard_map/adamw/pallas_call | solution.py:620
